TPU v7x, 256 devices: a 2x2x32 block of a 4x8x32 slice. The times are simulated.
256 devices in a mesh: grp: 4 (over y, x), row: 64 (over z, core).
Axes of the slice: x: 2, y: 2, z: 32, core: 2. Of those that a mesh axis runs over, the one named last changes fastest.
The devices are a block of a 4x8x32 slice.
Arguments:
- prior_basis: float32 [262144, 512], P(('grp', 'row')), parts along dimension 0, may hold values from -1 to 1, as said below
- samples: float32 [4, 262144, 64], P(None, ('grp', 'row')), parts along dimension 1, may hold values from -8 to 8
Outputs:
- new_basis: float32 [262144, 256], P(('grp', 'row')), parts along dimension 0
- leaf_estimates: float32 [4, 1024], P(None, ('grp', 'row')), parts along dimension 1
There are 4 independent parts, one for each index of `grp`. A program takes and returns all parts, laid end to end along the dimension named above; each array names one. Nothing has to cross between parts.
Inputs may be any that keep to these rules, and one draw needn't show every extreme that they name: The columns of prior_basis are orthonormal to float32 rounding.
All inputs are finite; a program needn't handle non-finite values.
Results may differ from a plain program's by a relative error of at most 0.0003.
Values sent between devices are 32-bit elements; how exact they have to be, the bound alone decides.
No kernel may reach another device: no remote copies, remote signals or barrier semaphores. Data moves between devices by JAX's collectives and lax.ppermute only.
A program may use at most 64 MiB of HBM per device.

v0:
```python
import functools

import jax
import jax.numpy as jnp
from jax import lax
from jax.sharding import Mesh
from jax.sharding import PartitionSpec as P

LEAF = 256
ROW = ("row_0", "row_1")
GRP_ROW = ("grp", "row_0", "row_1")


def over_axes(array, axes):
    return functools.reduce(lax.psum, axes, array)


def local(prior_basis, samples):
    highest = lax.Precision.HIGHEST
    rounds, local_rows, columns = samples.shape
    total_leaves = local_rows // LEAF * lax.axis_size(ROW)

    def energy_terms(block):
        return jnp.dot(block.T, block, precision=highest)

    prior_terms = jnp.einsum("nk,rns->rks", prior_basis, samples, precision=highest)
    stat_terms = jnp.stack([energy_terms(samples[number]) for number in range(rounds)])
    prior_all, stat_all = lax.psum((prior_terms, stat_terms), ROW)
    new_cols = []
    estimates = []
    for number in range(rounds):
        sample_block = samples[number]
        c_added = None
        if new_cols:
            added = jnp.concatenate(new_cols, axis=1)
        c_prior = prior_all[number]
        stat = stat_all[number]
        if new_cols:
            c_added = over_axes(jnp.dot(added.T, sample_block, precision=highest), ROW)
        remainder = sample_block - jnp.dot(prior_basis, c_prior, precision=highest)
        if new_cols:
            remainder = remainder - jnp.dot(added, c_added, precision=highest)
        gram = stat - jnp.dot(c_prior.T, c_prior, precision=highest)
        if new_cols:
            gram = gram - jnp.dot(c_added.T, c_added, precision=highest)
        energy = jnp.trace(stat)
        factor = jnp.linalg.cholesky(gram)
        fresh_cols = jax.scipy.linalg.solve_triangular(factor, remainder.T, lower=True).T
        leaf_energy = jnp.sum(
            (remainder * remainder).reshape(local_rows // LEAF, LEAF, columns), axis=(1, 2)
        )
        estimates.append(jnp.sqrt(total_leaves * leaf_energy / energy))
        new_cols.append(fresh_cols)
    return (jnp.concatenate(new_cols, axis=1), jnp.stack(estimates))


def solution(mesh):
    split = Mesh(mesh.devices.reshape(mesh.shape["grp"], 32, 2), ("grp", "row_0", "row_1"))
    in_specs = (P(GRP_ROW, None), P(None, GRP_ROW, None))
    out_specs = (P(GRP_ROW, None), P(None, GRP_ROW))
    return jax.shard_map(local, mesh=split, in_specs=in_specs, out_specs=out_specs, check_vma=False)
```

profile of v0, /device:TPU:37, one launch (start us, length us, event | category | flops | bytes accessed | tf_op | source)
XLA Modules:
  0.0 842.6 jit_solution(9579060003339560665)
XLA Ops:
  7.3 1.5 convolution_bitcast_fusion.8
  8.8 1.4 convolution_bitcast_fusion.9
  10.2 1.4 convolution_bitcast_fusion.10
  11.6 1.4 convolution_bitcast_fusion.7
  13.0 4.0 fusion.2
  17.0 0.6 pad_maximum_fusion.7
  17.8 400.5 %all-reduce.3.cloned.1.call-done = (f32[4,512,64]{1,2,0:T(8,128)}, f32[4,64,64]{1,2,0:T(8,128)}) async-done(((f32[4,512,64]{1,2,0:T(8,128)}, f32[4,64,64]{1,2,0:T(8,128)}), (f32[4,512,64]{1,2,0:T(8,128)}, f32[4,64,64]{1,2,0:T(8,128)})) %all-reduce.3.cloned.1.call-update) | async-done | bytes 589840 | tf_op jit(solution)/shard_map/psum | solution.py:28
  418.3 1.6 select_reduce_fusion.7
  419.8 1.2 convolution_subtract_fusion.9
  421.1 1.2 convolution_subtract_fusion.4
  422.3 1.2 convolution_subtract_fusion.6
  423.6 1.8 convolution_subtract_fusion.8
  425.4 3.7 fusion.5
  429.2 2.8 fusion.6
  432.0 2.8 fusion.7
  434.8 2.8 multiply_reduce_fusion.3
  437.7 0.1 copy.25
  437.8 5.8 cholesky.74
  443.6 0.6 compare_reduce_fusion.3
  444.3 0.7 fusion.31
  444.9 4.9 custom-call.8
  449.9 1.6 fusion.14
  451.4 0.4 fusion.20
  451.8 78.4 %psum.58 = f32[64,64]{1,0:T(8,128)S(1)} all-reduce(f32[64,64]{1,0:T(8,128)S(1)} %fusion.20), channel_id=1, replica_groups=mesh['grp'=4,'row_0'=32,'row_1'=2] {'row_0'}, use_global_device_ids=true, to_apply=%region_4.7 | all-reduce | flops 4096 | bytes 32768 | tf_op jit(solution)/shard_map/psum | solution.py:15
  530.2 31.0 %psum.59 = f32[64,64]{1,0:T(8,128)S(1)} all-reduce(f32[64,64]{1,0:T(8,128)S(1)} %psum.58), channel_id=1, replica_groups=mesh['grp'=4,'row_0'=32,'row_1'=2] {'row_1'}, use_global_device_ids=true, to_apply=%region_5.8 | all-reduce | flops 4096 | bytes 32768 | tf_op jit(solution)/shard_map/psum | solution.py:15
  561.2 1.0 convolution_subtract_fusion.7
  562.2 2.1 multiply_reduce_fusion.2
  564.3 0.1 reduce_sum.72
  564.5 0.1 reduce_sum.76
  564.6 0.6 fusion.40
  565.3 6.6 cholesky.85
  571.9 0.6 compare_reduce_fusion.2
  572.5 0.7 fusion.32
  573.2 4.9 custom-call.9
  578.1 1.4 convolution_bitcast_fusion.4
  579.5 0.7 copy-done.2
  580.2 0.7 fusion.10
  580.9 76.9 %psum.60 = f32[128,64]{0,1:T(8,128)S(1)} all-reduce(f32[128,64]{0,1:T(8,128)S(1)} %fusion.10), channel_id=1, replica_groups=mesh['grp'=4,'row_0'=32,'row_1'=2] {'row_0'}, use_global_device_ids=true, to_apply=%region_6.9 | all-reduce | flops 8192 | bytes 65536 | tf_op jit(solution)/shard_map/psum | solution.py:15
  657.8 31.0 %psum.61 = f32[128,64]{0,1:T(8,128)S(1)} all-reduce(f32[128,64]{0,1:T(8,128)S(1)} %psum.60), channel_id=1, replica_groups=mesh['grp'=4,'row_0'=32,'row_1'=2] {'row_1'}, use_global_device_ids=true, to_apply=%region_7.10 | all-reduce | flops 8192 | bytes 65536 | tf_op jit(solution)/shard_map/psum | solution.py:15
  688.8 0.2 convolution_subtract_fusion.5
  689.0 2.2 multiply_reduce_fusion.1
  691.1 0.1 reduce_sum.83
  691.4 5.8 cholesky.96
  697.2 0.6 compare_reduce_fusion.1
  697.9 0.7 fusion.33
  698.5 4.9 custom-call.10
  703.4 1.4 convolution_bitcast_fusion.2
  704.8 0.7 copy-done.3
  705.5 1.8 fusion.9
  707.3 76.7 %psum.62 = f32[192,64]{0,1:T(8,128)S(1)} all-reduce(f32[192,64]{0,1:T(8,128)S(1)} %fusion.9), channel_id=1, replica_groups=mesh['grp'=4,'row_0'=32,'row_1'=2] {'row_0'}, use_global_device_ids=true, to_apply=%region_8.11 | all-reduce | flops 12288 | bytes 98304 | tf_op jit(solution)/shard_map/psum | solution.py:15
  784.0 31.4 %psum.63 = f32[192,64]{0,1:T(8,128)S(1)} all-reduce(f32[192,64]{0,1:T(8,128)S(1)} %psum.62), channel_id=1, replica_groups=mesh['grp'=4,'row_0'=32,'row_1'=2] {'row_1'}, use_global_device_ids=true, to_apply=%region_9.12 | all-reduce | flops 12288 | bytes 98304 | tf_op jit(solution)/shard_map/psum | solution.py:15
  815.4 0.2 convolution_subtract_fusion.3
  815.6 1.7 multiply_reduce_fusion
  817.4 0.1 reduce_sum.106
  817.6 5.8 cholesky.107
  823.5 0.6 compare_reduce_fusion
  824.2 0.7 fusion.34
  824.8 4.9 custom-call.11
  829.7 0.4 convolution_bitcast_fusion
  830.1 1.1 pad_maximum_fusion
  831.3 1.3 copy.35
  832.6 1.3 sqrt_bitcast_fusion.2
  833.9 1.3 sqrt_bitcast_fusion
  835.1 0.6 pad_maximum_fusion.8
  (24 shorter events, 0.5 us)
Async XLA Ops:
  7.2 5.8 copy-start
  7.2 411.1 %all-reduce.3.cloned.1.call-start = ((), (), s32[]{:S(2)}) async-start(), calls=%async_computation | async-start | bytes 1310720 | tf_op jit(solution)/shard_map/psum | solution.py:28
  13.0 412.4 %copy-start.1 = (f32[4,1024,64]{1,2,0:T(8,128)S(1)}, f32[4,1024,64]{1,2,0:T(8,128)}, u32[]{:S(2)}) copy-start(f32[4,1024,64]{1,2,0:T(8,128)} %param.6) | copy-start | bytes 3145732
  418.3 10.9 %copy-start.4 = (f32[4,512,64]{1,2,0:T(8,128)S(1)}, f32[4,512,64]{1,2,0:T(8,128)}, u32[]{:S(2)}) copy-start(f32[4,512,64]{1,2,0:T(8,128)} %get-tuple-element.12) | copy-start | bytes 1572868
  579.5 0.7 copy-start.2
  704.8 0.7 copy-start.3
Sparse Core Ops, SparseCore 0:
  17.9 400.3 all-reduce.2
where the time goes:
time: 843 us
  waiting for transfers between devices  401 us (48%)
  blocking collectives  325 us (39%)
  other arithmetic  56.6 us (7%)
  matrix products  42.5 us (5%)
  between operations  14.4 us (2%)
    psum x1, waiting for transfers between devices, local(): prior_all, stat_all = lax.psum((prior_terms, stat_terms), ROW)  401 us
    psum x6, blocking collectives, over_axes(): return functools.reduce(lax.psum, axes, array)  325 us
    another operation x12, other arithmetic, local(): factor = jnp.linalg.cholesky(gram)  26.8 us
    another operation x8, other arithmetic, local(): jax.scipy.linalg.solve_triangular(factor, remainder.T, lower=True)  22.2 us
  transfers between devices with their start and end apart: 1, of which 1 were waited for; matrix products, arithmetic and copies ran while one was open for 0% of the time, Pallas kernels for 0%

commit v1 on v0

v1 whole, which is shorter than its diff:
```python
import functools

import jax
import jax.numpy as jnp
from jax import lax
from jax.experimental import pallas as pl
from jax.experimental.pallas import tpu as pltpu
from jax.sharding import Mesh
from jax.sharding import PartitionSpec as P

LEAF = 256
LANES = 128
NEAR = 4
CORES = 2
ROW = ("far", "near", "core")
GRP_ROW = ("grp",) + ROW
NT = (((1,), (1,)), ((), ()))
TN = (((0,), (0,)), ((), ()))
NN = (((1,), (0,)), ((), ()))


def split(x):
    high = x.astype(jnp.bfloat16)
    low = (x - high.astype(jnp.float32)).astype(jnp.bfloat16)
    return high, low


def dot3(a, b, dims):
    dot = functools.partial(lax.dot_general, dimension_numbers=dims, preferred_element_type=jnp.float32)
    return dot(a[0], b[0]) + (dot(a[0], b[1]) + dot(a[1], b[0]))


def dot_full(a, b, dims):
    return lax.dot_general(a, b, dims, precision=lax.Precision.HIGHEST, preferred_element_type=jnp.float32)


def stats_kernel(core_ref, q_ref, y_ref, mine_ref, theirs_ref, y_out_ref, acc_ref):
    step = pl.program_id(0)
    y = jnp.concatenate([y_ref[r] for r in range(y_ref.shape[0])], axis=1)
    y_out_ref[...] = y
    basis = q_ref.shape[1]
    half = y.shape[1] // CORES
    ys = split(y)
    qs = split(q_ref[...])
    with_basis = dot3(ys, qs, TN)
    with_self = dot3(ys, ys, TN) + lax.dot_general(ys[1], ys[1], TN, preferred_element_type=jnp.float32)

    @pl.when(step == 0)
    def _():
        acc_ref[...] = jnp.zeros_like(acc_ref)

    for c in range(CORES):
        rows = slice(c * half, (c + 1) * half)
        acc_ref[c, :, :basis] += with_basis[rows]
        acc_ref[c, :, basis:] += with_self[rows]

    @pl.when(step == pl.num_programs(0) - 1)
    def _():
        core = core_ref[0]
        for block in range(acc_ref.shape[2] // LANES):
            lanes = slice(block * LANES, (block + 1) * LANES)
            rows = slice(block * half, (block + 1) * half)
            mine_ref[rows, :] = acc_ref[core, :, lanes]
            theirs_ref[rows, :] = acc_ref[1 - core, :, lanes]


def factor_block(block):
    size = block.shape[0]
    row_at = lax.broadcasted_iota(jnp.int32, (size, size), 0)
    lane_at = lax.broadcasted_iota(jnp.int32, (size, size), 1)
    eye = (row_at == lane_at).astype(jnp.float32)
    work = jnp.concatenate([block, eye], axis=1)
    width = 2 * size
    parts = [work[8 * i:8 * i + 8] for i in range(size // 8)]
    sub = lax.broadcasted_iota(jnp.int32, (8, width), 0)
    pivots = []
    for j in range(size):
        at, inner = divmod(j, 8)
        columns = [jnp.broadcast_to(part[:, j:j + 1], (8, width)) for part in parts[at:]]
        pivot = jnp.broadcast_to(columns[0][inner:inner + 1], (8, width))
        row = jnp.broadcast_to(parts[at][inner:inner + 1], (8, width))
        pivots.append(pivot)
        scaled = row * (1.0 / pivot)
        if inner < 7:
            parts[at] = parts[at] - jnp.where(sub > inner, columns[0], 0.0) * scaled
        for i in range(at + 1, len(parts)):
            parts[i] = parts[i] - columns[i - at] * scaled
    scales = []
    for at in range(len(parts)):
        scale = pivots[8 * at]
        for inner in range(1, 8):
            scale = jnp.where(sub == inner, pivots[8 * at + inner], scale)
        scales.append(lax.rsqrt(scale))
    done = jnp.concatenate([part * scale for part, scale in zip(parts, scales)], axis=0)
    upper = jnp.where(row_at <= lane_at, done[:, :size], 0.0)
    return upper, done[:, size:]


def finish_kernel(leaves, sums_ref, q_hbm, y_hbm, v_ref, est_ref, q_ref, y_ref, work_ref, sems):
    q_copy = pltpu.make_async_copy(q_hbm, q_ref, sems.at[0])
    y_copy = pltpu.make_async_copy(y_hbm, y_ref, sems.at[1])
    q_copy.start()
    y_copy.start()
    rows, basis = q_ref.shape
    columns = y_ref.shape[1]
    rounds = est_ref.shape[0]
    size = columns // rounds
    half = columns // CORES

    def lanes_block(block):
        return jnp.concatenate([sums_ref[c, block * half:(block + 1) * half, :] for c in range(CORES)], axis=0)

    coefs = jnp.concatenate([lanes_block(b) for b in range(basis // LANES)], axis=1)
    own = jnp.concatenate([lanes_block(basis // LANES + b) for b in range(columns // LANES)], axis=1)
    row_at = lax.broadcasted_iota(jnp.int32, (columns, columns), 0)
    lane_at = lax.broadcasted_iota(jnp.int32, (columns, columns), 1)
    work_ref[:, :columns] = own - dot_full(coefs, coefs, NT)
    work_ref[:, columns:] = (row_at == lane_at).astype(jnp.float32)
    uppers = []
    for k in range(rounds):
        here = slice(k * size, (k + 1) * size)
        after = slice((k + 1) * size, columns)
        upper, inverse = factor_block(work_ref[here, here])
        uppers.append(upper)
        done = dot_full(inverse, work_ref[here, :], NN)
        work_ref[here, :] = done
        if k + 1 < rounds:
            work_ref[after, :] -= dot_full(done[:, after], done, TN)
    zero = jnp.zeros((size, size), jnp.float32)
    diagonal = jnp.concatenate(
        [jnp.concatenate([uppers[k] if j == k else zero for j in range(rounds)], axis=1) for k in range(rounds)], axis=0
    )
    inverse = work_ref[:, columns:]
    inverse_t = split(jnp.where(row_at >= lane_at, inverse, 0.0))
    diagonal_s = split(diagonal)
    coefs_s = split(coefs)
    q_copy.wait()
    y_copy.wait()
    sums = []
    for leaf in range(rows // LEAF):
        span = slice(leaf * LEAF, (leaf + 1) * LEAF)
        projected = y_ref[span, :] - dot3(split(q_ref[span, :]), coefs_s, NT)
        fresh = dot3(split(projected), inverse_t, NT)
        v_ref[span, :] = fresh
        remainder = dot3(split(fresh), diagonal_s, NN)
        sums.append(jnp.sum(remainder * remainder, axis=0, keepdims=True))
    count = len(sums)
    member = (
        lax.broadcasted_iota(jnp.int32, (8, columns), 0)
        == lax.broadcasted_iota(jnp.int32, (8, columns), 1) // size
    ).astype(jnp.float32)
    leaf_energy = dot_full(member, jnp.concatenate(sums + [jnp.zeros((8 - count, columns), jnp.float32)], axis=0), NT)
    energies = jnp.sum(jnp.where(row_at == lane_at, own, 0.0), axis=0, keepdims=True)
    energy = jnp.sum(member * energies, axis=1, keepdims=True)
    est_ref[...] = jnp.sqrt(leaves * leaf_energy / energy)[:rounds, :count]


def local(prior_basis, samples):
    rounds, rows, size = samples.shape
    basis = prior_basis.shape[1]
    columns = rounds * size
    half = columns // CORES
    depth = (basis + columns) // LANES * half
    far = lax.axis_size("far")
    core = lax.axis_index("core").reshape(1).astype(jnp.int32)
    step = LEAF
    mine, theirs, samples_wide = pl.pallas_call(
        stats_kernel,
        grid=(rows // step,),
        in_specs=[
            pl.BlockSpec(memory_space=pltpu.SMEM),
            pl.BlockSpec((step, basis), lambda i: (i, 0)),
            pl.BlockSpec((rounds, step, size), lambda i: (0, i, 0)),
        ],
        out_specs=[
            pl.BlockSpec((depth, LANES), lambda i: (0, 0)),
            pl.BlockSpec((depth, LANES), lambda i: (0, 0)),
            pl.BlockSpec((step, columns), lambda i: (i, 0)),
        ],
        out_shape=[
            jax.ShapeDtypeStruct((depth, LANES), jnp.float32),
            jax.ShapeDtypeStruct((depth, LANES), jnp.float32),
            jax.ShapeDtypeStruct((rows, columns), jnp.float32),
        ],
        scratch_shapes=[pltpu.VMEM((CORES, half, basis + columns), jnp.float32)],
        name="stats",
    )(core, prior_basis, samples)
    chip = mine + lax.ppermute(theirs, "core", [(0, 1), (1, 0)])
    near_parts = lax.all_to_all(chip.reshape(NEAR, depth // NEAR, LANES), "near", 0, 0, tiled=True)
    near_sum = jnp.sum(near_parts, axis=0).reshape(far, depth // NEAR // far, LANES)
    far_parts = lax.all_to_all(near_sum, "far", 0, 0, tiled=True)
    total = jnp.sum(far_parts, axis=0)
    far_all = lax.all_to_all(jnp.broadcast_to(total, far_parts.shape), "far", 0, 0, tiled=True)
    sums = lax.all_gather(far_all.reshape(1, depth // NEAR, LANES), ("core", "near"), axis=0, tiled=True)
    sums = sums.reshape(CORES, depth, LANES)
    leaves = rows // LEAF * far * NEAR * CORES
    return pl.pallas_call(
        functools.partial(finish_kernel, float(leaves)),
        in_specs=[
            pl.BlockSpec(memory_space=pltpu.VMEM),
            pl.BlockSpec(memory_space=pl.ANY),
            pl.BlockSpec(memory_space=pl.ANY),
        ],
        out_specs=[pl.BlockSpec(memory_space=pltpu.VMEM), pl.BlockSpec(memory_space=pltpu.VMEM)],
        out_shape=[
            jax.ShapeDtypeStruct((rows, columns), jnp.float32),
            jax.ShapeDtypeStruct((rounds, rows // LEAF), jnp.float32),
        ],
        scratch_shapes=[
            pltpu.VMEM((rows, basis), jnp.float32),
            pltpu.VMEM((rows, columns), jnp.float32),
            pltpu.VMEM((columns, 2 * columns), jnp.float32),
            pltpu.SemaphoreType.DMA((2,)),
        ],
        name="finish",
    )(sums, prior_basis, samples_wide)


def solution(mesh):
    grp = mesh.shape["grp"]
    far = mesh.shape["row"] // (NEAR * CORES)
    parts = Mesh(mesh.devices.reshape(grp, far, NEAR, CORES), GRP_ROW)
    in_specs = (P(GRP_ROW, None), P(None, GRP_ROW, None))
    out_specs = (P(GRP_ROW, None), P(None, GRP_ROW))
    return jax.shard_map(local, mesh=parts, in_specs=in_specs, out_specs=out_specs, check_vma=False)
```

time: 843 us -> 188 us (0.22)
  waiting for transfers between devices: 401 us -> 1.56 us
  blocking collectives: 325 us -> 112 us
  other arithmetic: 56.6 us -> 1.09 us
  Pallas kernels: 0 us -> 48.6 us
  matrix products: 42.5 us -> 0 us
  starting transfers between devices: 0.06 us -> 20.4 us
  between operations: 14.4 us -> 0.65 us
    psum x1 -> x0, waiting for transfers between devices: 401 us -> none  [local(): prior_all, stat_all = lax.psum((prior_terms, stat_terms), ROW)]
    psum x6 -> x0, blocking collectives: 325 us -> none  [over_axes(): return functools.reduce(lax.psum, axes, array)]
    all_to_all x0 -> x3, blocking collectives: none -> 78.4 us  [the longest x1 35.9 us: local(): far_parts = lax.all_to_all(near_sum, 'far', 0, 0, tiled=True)]
    another operation x22 -> x0, other arithmetic: 50.3 us -> none  [the longest x12 26.8 us: local(): factor = jnp.linalg.cholesky(gram)]
    pallas_call x0 -> x2, Pallas kernels: none -> 48.6 us  [the longest x1 42.8 us: local(): pl.pallas_call(functools.partial(finish_kernel, float(leaves)), in_specs=...]
    dot_general x22 -> x0, matrix products: 37.7 us -> none  [the longest x4 12.2 us: local(): remainder = sample_block - jnp.dot(prior_basis, c_prior, precision=highest)]
    all_gather x0 -> x1, blocking collectives: none -> 33.6 us  [local(): lax.all_gather(far_all.reshape(1, depth // NEAR, LANES), ('core', 'near')...]
    ppermute x0 -> x1, starting transfers between devices: none -> 20.4 us  [local(): chip = mine + lax.ppermute(theirs, 'core', [(0, 1), (1, 0)])]
where the time goes in v1:
time: 188 us
  blocking collectives  112 us (60%)
  Pallas kernels  48.6 us (26%)
  starting transfers between devices  20.4 us (11%)
  local copies, waits for them, and re-layouts  3.19 us (2%)
    pallas_call x1, Pallas kernels, local(): pl.pallas_call(functools.partial(finish_kernel, float(leaves)), in_specs=...  42.8 us
    all_to_all x1, blocking collectives, local(): far_parts = lax.all_to_all(near_sum, 'far', 0, 0, tiled=True)  35.9 us
    all_gather x1, blocking collectives, local(): lax.all_gather(far_all.reshape(1, depth // NEAR, LANES), ('core', 'near')...  33.6 us
    all_to_all x1, blocking collectives, local(): lax.all_to_all(jnp.broadcast_to(total, far_parts.shape), 'far', 0, 0, til...  28.7 us
    ppermute x1, starting transfers between devices, local(): chip = mine + lax.ppermute(theirs, 'core', [(0, 1), (1, 0)])  20.4 us
    all_to_all x1, blocking collectives, local(): lax.all_to_all(chip.reshape(NEAR, depth // NEAR, LANES), 'near', 0, 0, ti...  13.8 us
    pallas_call x1, Pallas kernels, local(): pl.pallas_call(stats_kernel, grid=(rows // step,), in_specs=[pl.BlockSpec...  5.83 us
  transfers between devices with their start and end apart: 1, of which 1 were waited for; matrix products, arithmetic and copies ran while one was open for 0% of the time, Pallas kernels for 0%

profile of v1, /device:TPU:37, one launch (start us, length us, event | category | flops | bytes accessed | tf_op | source)
XLA Modules:
  0.0 187.5 jit_solution(16860954856755048357)
XLA Ops:
  0.6 3.2 %copy.6.y_ref = f32[4,1024,64]{2,1,0:T(8,128)} copy(f32[4,1024,64]{1,2,0:T(8,128)} %param.3) | data formatting | bytes 2097152 | tf_op args[1]
  3.8 5.8 %stats.1 = (f32[768,128]{1,0:T(8,128)}, f32[768,128]{1,0:T(8,128)}, f32[1024,256]{1,0:T(8,128)}) custom-call(s32[1]{0:T(128)} %bitcast.core_ref, f32[1024,512]{1,0:T(8,128)} %q_hbm.1, f32[4,1024,64]{2,1,0:T(8,128)} %copy.6.y_ref), custom_call_target="tpu_custom_call" | custom-call | tf_op jit(solution)/shard_map/stats/pallas_call | solution.py:167
  9.7 20.4 %collective-permute-start = (f32[768,128]{1,0:T(8,128)}, f32[768,128]{1,0:T(8,128)S(1)}, u32[]{:S(2)}, u32[]{:S(2)}) collective-permute-start(f32[768,128]{1,0:T(8,128)} %get-tuple-element.6), channel_id=1, source_target_pairs={{0,1},{1,0},{2,3},{3,2},{4,5},{5,4},{6,7},{7,6},{8,9},{9,8},{10,11... | collective-permute-start | bytes 1179656 | tf_op jit(solution)/shard_map/ppermute | solution.py:188
  30.1 1.6 collective-permute-done
  31.6 1.1 add.3
  32.7 13.8 %all_to_all.15 = f32[4,192,128]{2,1,0:T(8,128)S(1)} all-to-all(f32[4,192,128]{2,1,0:T(8,128)S(1)} %bitcast.6), channel_id=1, replica_groups=mesh['grp'=4,'far'=8,'near'=4,'core'=2] {'near'}, dimensions={0} | all-to-all | bytes 786432 | tf_op jit(solution)/shard_map/all_to_all | solution.py:189
  46.5 35.9 %all_to_all.16 = f32[8,24,128]{2,1,0:T(8,128)S(1)} all-to-all(f32[8,24,128]{2,1,0:T(8,128)S(1)} %bitcast.8), channel_id=1, replica_groups=mesh['grp'=4,'far'=8,'near'=4,'core'=2] {'far'}, dimensions={0} | all-to-all | bytes 196608 | tf_op jit(solution)/shard_map/all_to_all | solution.py:191
  82.5 28.7 %all_to_all.17 = f32[8,24,128]{2,1,0:T(8,128)S(1)} all-to-all(f32[8,24,128]{2,1,0:T(8,128)S(1)} %broadcast_in_dim.3), channel_id=1, replica_groups=mesh['grp'=4,'far'=8,'near'=4,'core'=2] {'far'}, dimensions={0} | all-to-all | bytes 196608 | tf_op jit(solution)/shard_map/all_to_all | solution.py:193
  111.2 33.6 %all_gather.3 = f32[8,192,128]{2,1,0:T(8,128)} all-gather(f32[1,192,128]{2,1,0:T(8,128)S(1)} %bitcast.7), channel_id=1, replica_groups=mesh['grp'=4,'far'=8,'near'=4,'core'=2] {'core','near'}, dimensions={0}, use_global_device_ids=true | all-gather | bytes 884736 | tf_op jit(solution)/shard_map/all_gather | solution.py:194
  144.7 42.8 %finish.1 = (f32[1024,256]{1,0:T(8,128)}, f32[4,4]{1,0:T(4,128)}) custom-call(f32[2,768,128]{2,1,0:T(8,128)} %bitcast.5, f32[1024,512]{1,0:T(8,128)} %q_hbm.1, f32[1024,256]{1,0:T(8,128)} %get-tuple-element.7.y_hbm), custom_call_target="tpu_custom_call" | custom-call | tf_op jit(solution)/shard_map/finish/pallas_call | solution.py:197
  (3 shorter events, 0.0 us)
Async XLA Ops:
  9.7 22.0 %collective-permute-start = (f32[768,128]{1,0:T(8,128)}, f32[768,128]{1,0:T(8,128)S(1)}, u32[]{:S(2)}, u32[]{:S(2)}) collective-permute-start(f32[768,128]{1,0:T(8,128)} %get-tuple-element.6), channel_id=1, source_target_pairs={{0,1},{1,0},{2,3},{3,2},{4,5},{5,4},{6,7},{7,6},{8,9},{9,8},{10,11... | collective-permute-start | bytes 1179656 | tf_op jit(solution)/shard_map/ppermute | solution.py:188

commit v2 on v1

--- a/solution.py
+++ b/solution.py
@@ -1,4 +1,5 @@
 import functools
+import math
 
 import jax
 import jax.numpy as jnp
@@ -34,16 +35,14 @@
     return lax.dot_general(a, b, dims, precision=lax.Precision.HIGHEST, preferred_element_type=jnp.float32)
 
 
-def stats_kernel(core_ref, q_ref, y_ref, mine_ref, theirs_ref, y_out_ref, acc_ref):
+def stats_kernel(core_ref, q_ref, yt_ref, mine_ref, theirs_ref, acc_ref):
     step = pl.program_id(0)
-    y = jnp.concatenate([y_ref[r] for r in range(y_ref.shape[0])], axis=1)
-    y_out_ref[...] = y
+    yt = yt_ref[...].reshape(-1, yt_ref.shape[2])
     basis = q_ref.shape[1]
-    half = y.shape[1] // CORES
-    ys = split(y)
-    qs = split(q_ref[...])
-    with_basis = dot3(ys, qs, TN)
-    with_self = dot3(ys, ys, TN) + lax.dot_general(ys[1], ys[1], TN, preferred_element_type=jnp.float32)
+    half = yt.shape[0] // CORES
+    ys = split(yt)
+    with_basis = dot3(ys, split(q_ref[...]), NN)
+    with_self = dot3(ys, ys, NT) + lax.dot_general(ys[1], ys[1], NT, preferred_element_type=jnp.float32)
 
     @pl.when(step == 0)
     def _():
@@ -64,6 +63,10 @@
             theirs_ref[rows, :] = acc_ref[1 - core, :, lanes]
 
 
+def spread_row(x, r):
+    return jnp.broadcast_to(x[r:r + 1], x.shape)
+
+
 def factor_block(block):
     size = block.shape[0]
     row_at = lax.broadcasted_iota(jnp.int32, (size, size), 0)
@@ -71,44 +74,66 @@
     eye = (row_at == lane_at).astype(jnp.float32)
     work = jnp.concatenate([block, eye], axis=1)
     width = 2 * size
-    parts = [work[8 * i:8 * i + 8] for i in range(size // 8)]
+    count = size // 8
+    parts = [work[8 * i:8 * i + 8] for i in range(count)]
     sub = lax.broadcasted_iota(jnp.int32, (8, width), 0)
-    pivots = []
-    for j in range(size):
-        at, inner = divmod(j, 8)
-        columns = [jnp.broadcast_to(part[:, j:j + 1], (8, width)) for part in parts[at:]]
-        pivot = jnp.broadcast_to(columns[0][inner:inner + 1], (8, width))
-        row = jnp.broadcast_to(parts[at][inner:inner + 1], (8, width))
-        pivots.append(pivot)
-        scaled = row * (1.0 / pivot)
-        if inner < 7:
-            parts[at] = parts[at] - jnp.where(sub > inner, columns[0], 0.0) * scaled
-        for i in range(at + 1, len(parts)):
-            parts[i] = parts[i] - columns[i - at] * scaled
-    scales = []
-    for at in range(len(parts)):
-        scale = pivots[8 * at]
-        for inner in range(1, 8):
-            scale = jnp.where(sub == inner, pivots[8 * at + inner], scale)
-        scales.append(lax.rsqrt(scale))
-    done = jnp.concatenate([part * scale for part, scale in zip(parts, scales)], axis=0)
+    done = []
+    for p in range(count):
+        cols = [
+            [jnp.take_along_axis(parts[i], jnp.full((8, width), 8 * p + m, jnp.int32), axis=1) for m in range(8)]
+            for i in range(p, count)
+        ]
+        own = cols[0]
+        pivots = None
+        steps = []
+        for m in range(8):
+            pivot = spread_row(own[m], m)
+            pivots = pivot if m == 0 else jnp.where(sub == m, pivot, pivots)
+            inverse = 1.0 / pivot
+            row = spread_row(parts[p], m) * inverse
+            entries = {k: spread_row(own[k], m) * inverse for k in range(m + 1, 8)}
+            steps.append((row, entries))
+            if m < 7:
+                below = jnp.where(sub > m, own[m], 0.0)
+                for k in range(m + 1, 8):
+                    own[k] = own[k] - below * entries[k]
+                parts[p] = parts[p] - below * row
+        done.append(parts[p] * lax.rsqrt(pivots))
+        for i in range(p + 1, count):
+            col = cols[i - p]
+            for m, (row, entries) in enumerate(steps):
+                parts[i] = parts[i] - col[m] * row
+                for k in range(m + 1, 8):
+                    col[k] = col[k] - col[m] * entries[k]
+    done = jnp.concatenate(done, axis=0)
     upper = jnp.where(row_at <= lane_at, done[:, :size], 0.0)
     return upper, done[:, size:]
 
 
-def finish_kernel(leaves, sums_ref, q_hbm, y_hbm, v_ref, est_ref, q_ref, y_ref, work_ref, sems):
+def finish_kernel(leaves, sums_ref, q_hbm, yt_hbm, v_ref, est_ref, q_ref, yt_ref, work_ref, sems):
     q_copy = pltpu.make_async_copy(q_hbm, q_ref, sems.at[0])
-    y_copy = pltpu.make_async_copy(y_hbm, y_ref, sems.at[1])
+    y_copy = pltpu.make_async_copy(yt_hbm, yt_ref, sems.at[1])
     q_copy.start()
     y_copy.start()
     rows, basis = q_ref.shape
-    columns = y_ref.shape[1]
+    columns = yt_ref.shape[0] * yt_ref.shape[1]
     rounds = est_ref.shape[0]
     size = columns // rounds
     half = columns // CORES
 
+    unit_rows = math.gcd(half, sums_ref.shape[2])
+    units_near = sums_ref.shape[2] // unit_rows
+
     def lanes_block(block):
-        return jnp.concatenate([sums_ref[c, block * half:(block + 1) * half, :] for c in range(CORES)], axis=0)
+        units = [divmod(unit, units_near) for unit in range(block * half // unit_rows, (block + 1) * half // unit_rows)]
+        return jnp.concatenate(
+            [
+                sums_ref[near, c, part * unit_rows:(part + 1) * unit_rows, :]
+                for c in range(CORES)
+                for near, part in units
+            ],
+            axis=0,
+        )
 
     coefs = jnp.concatenate([lanes_block(b) for b in range(basis // LANES)], axis=1)
     own = jnp.concatenate([lanes_block(basis // LANES + b) for b in range(columns // LANES)], axis=1)
@@ -139,7 +164,8 @@
     sums = []
     for leaf in range(rows // LEAF):
         span = slice(leaf * LEAF, (leaf + 1) * LEAF)
-        projected = y_ref[span, :] - dot3(split(q_ref[span, :]), coefs_s, NT)
+        samples = yt_ref[:, :, span].reshape(columns, LEAF).T
+        projected = samples - dot3(split(q_ref[span, :]), coefs_s, NT)
         fresh = dot3(split(projected), inverse_t, NT)
         v_ref[span, :] = fresh
         remainder = dot3(split(fresh), diagonal_s, NN)
@@ -164,35 +190,34 @@
     far = lax.axis_size("far")
     core = lax.axis_index("core").reshape(1).astype(jnp.int32)
     step = LEAF
-    mine, theirs, samples_wide = pl.pallas_call(
+    samples_t = jnp.transpose(samples, (0, 2, 1))
+    mine, theirs = pl.pallas_call(
         stats_kernel,
         grid=(rows // step,),
         in_specs=[
             pl.BlockSpec(memory_space=pltpu.SMEM),
             pl.BlockSpec((step, basis), lambda i: (i, 0)),
-            pl.BlockSpec((rounds, step, size), lambda i: (0, i, 0)),
+            pl.BlockSpec((rounds, size, step), lambda i: (0, 0, i)),
         ],
         out_specs=[
             pl.BlockSpec((depth, LANES), lambda i: (0, 0)),
             pl.BlockSpec((depth, LANES), lambda i: (0, 0)),
-            pl.BlockSpec((step, columns), lambda i: (i, 0)),
         ],
         out_shape=[
             jax.ShapeDtypeStruct((depth, LANES), jnp.float32),
             jax.ShapeDtypeStruct((depth, LANES), jnp.float32),
-            jax.ShapeDtypeStruct((rows, columns), jnp.float32),
         ],
         scratch_shapes=[pltpu.VMEM((CORES, half, basis + columns), jnp.float32)],
         name="stats",
-    )(core, prior_basis, samples)
+    )(core, prior_basis, samples_t)
     chip = mine + lax.ppermute(theirs, "core", [(0, 1), (1, 0)])
     near_parts = lax.all_to_all(chip.reshape(NEAR, depth // NEAR, LANES), "near", 0, 0, tiled=True)
     near_sum = jnp.sum(near_parts, axis=0).reshape(far, depth // NEAR // far, LANES)
     far_parts = lax.all_to_all(near_sum, "far", 0, 0, tiled=True)
     total = jnp.sum(far_parts, axis=0)
     far_all = lax.all_to_all(jnp.broadcast_to(total, far_parts.shape), "far", 0, 0, tiled=True)
-    sums = lax.all_gather(far_all.reshape(1, depth // NEAR, LANES), ("core", "near"), axis=0, tiled=True)
-    sums = sums.reshape(CORES, depth, LANES)
+    sums = lax.all_gather(far_all.reshape(1, depth // NEAR, LANES), ("near", "core"), axis=0, tiled=True)
+    sums = sums.reshape(NEAR, CORES, depth // NEAR, LANES)
     leaves = rows // LEAF * far * NEAR * CORES
     return pl.pallas_call(
         functools.partial(finish_kernel, float(leaves)),
@@ -208,12 +233,12 @@
         ],
         scratch_shapes=[
             pltpu.VMEM((rows, basis), jnp.float32),
-            pltpu.VMEM((rows, columns), jnp.float32),
+            pltpu.VMEM((rounds, size, rows), jnp.float32),
             pltpu.VMEM((columns, 2 * columns), jnp.float32),
             pltpu.SemaphoreType.DMA((2,)),
         ],
         name="finish",
-    )(sums, prior_basis, samples_wide)
+    )(sums, prior_basis, samples_t)
 
 
 def solution(mesh):

time: 188 us -> 141 us (0.75)
  Pallas kernels: 48.6 us -> 18.8 us
  blocking collectives: 112 us -> 98.3 us
  local copies, waits for them, and re-layouts: 3.19 us -> 0.01 us
    pallas_call x1, Pallas kernels: 42.8 us -> 13.8 us  [local(): pl.pallas_call(functools.partial(finish_kernel, float(leaves)), in_specs=...]
    all_gather x1, blocking collectives: 33.6 us -> 19.9 us  [local(): lax.all_gather(far_all.reshape(1, depth // NEAR, LANES), ('near', 'core')...]
    unnamed x1 -> x0, local copies, waits for them, and re-layouts: 3.19 us -> none
where the time goes in v2:
time: 141 us
  blocking collectives  98.3 us (70%)
  starting transfers between devices  20.4 us (14%)
  Pallas kernels  18.8 us (13%)
  waiting for transfers between devices  1.56 us (1%)
    all_to_all x1, blocking collectives, local(): far_parts = lax.all_to_all(near_sum, 'far', 0, 0, tiled=True)  35.9 us
    all_to_all x1, blocking collectives, local(): lax.all_to_all(jnp.broadcast_to(total, far_parts.shape), 'far', 0, 0, til...  28.7 us
    ppermute x1, starting transfers between devices, local(): chip = mine + lax.ppermute(theirs, 'core', [(0, 1), (1, 0)])  20.4 us
    all_gather x1, blocking collectives, local(): lax.all_gather(far_all.reshape(1, depth // NEAR, LANES), ('near', 'core')...  19.9 us
    all_to_all x1, blocking collectives, local(): lax.all_to_all(chip.reshape(NEAR, depth // NEAR, LANES), 'near', 0, 0, ti...  13.8 us
    pallas_call x1, Pallas kernels, local(): pl.pallas_call(functools.partial(finish_kernel, float(leaves)), in_specs=...  13.8 us
    pallas_call x1, Pallas kernels, local(): pl.pallas_call(stats_kernel, grid=(rows // step,), in_specs=[pl.BlockSpec...  5.05 us
  transfers between devices with their start and end apart: 1, of which 1 were waited for; matrix products, arithmetic and copies ran while one was open for 0% of the time, Pallas kernels for 0%

profile of v2, /device:TPU:37, one launch (start us, length us, event | category | flops | bytes accessed | tf_op | source)
XLA Modules:
  0.0 140.8 jit_solution(3021363571403929745)
XLA Ops:
  0.6 5.1 %stats.1 = (f32[768,128]{1,0:T(8,128)}, f32[768,128]{1,0:T(8,128)}) custom-call(s32[1]{0:T(128)} %bitcast.core_ref, f32[1024,512]{1,0:T(8,128)} %q_hbm.1, f32[4,64,1024]{2,1,0:T(8,128)} %bitcast.6), custom_call_target="tpu_custom_call" | custom-call | tf_op jit(solution)/shard_map/stats/pallas_call | solution.py:194
  5.7 20.4 %collective-permute-start = (f32[768,128]{1,0:T(8,128)}, f32[768,128]{1,0:T(8,128)S(1)}, u32[]{:S(2)}, u32[]{:S(2)}) collective-permute-start(f32[768,128]{1,0:T(8,128)} %get-tuple-element.5), channel_id=1, source_target_pairs={{0,1},{1,0},{2,3},{3,2},{4,5},{5,4},{6,7},{7,6},{8,9},{9,8},{10,11... | collective-permute-start | bytes 1179656 | tf_op jit(solution)/shard_map/ppermute | solution.py:213
  26.1 1.6 %collective-permute-done = f32[768,128]{1,0:T(8,128)S(1)} collective-permute-done((f32[768,128]{1,0:T(8,128)}, f32[768,128]{1,0:T(8,128)S(1)}, u32[]{:S(2)}, u32[]{:S(2)}) %collective-permute-start) | collective-permute-done | bytes 393248 | tf_op jit(solution)/shard_map/ppermute | solution.py:213
  27.7 1.1 add.3
  28.7 13.8 %all_to_all.15 = f32[4,192,128]{2,1,0:T(8,128)S(1)} all-to-all(f32[4,192,128]{2,1,0:T(8,128)S(1)} %bitcast.9), channel_id=1, replica_groups=mesh['grp'=4,'far'=8,'near'=4,'core'=2] {'near'}, dimensions={0} | all-to-all | bytes 786432 | tf_op jit(solution)/shard_map/all_to_all | solution.py:214
  42.6 35.9 %all_to_all.16 = f32[8,24,128]{2,1,0:T(8,128)S(1)} all-to-all(f32[8,24,128]{2,1,0:T(8,128)S(1)} %bitcast.11), channel_id=1, replica_groups=mesh['grp'=4,'far'=8,'near'=4,'core'=2] {'far'}, dimensions={0} | all-to-all | bytes 196608 | tf_op jit(solution)/shard_map/all_to_all | solution.py:216
  78.5 28.7 %all_to_all.17 = f32[8,24,128]{2,1,0:T(8,128)S(1)} all-to-all(f32[8,24,128]{2,1,0:T(8,128)S(1)} %broadcast_in_dim.3), channel_id=1, replica_groups=mesh['grp'=4,'far'=8,'near'=4,'core'=2] {'far'}, dimensions={0} | all-to-all | bytes 196608 | tf_op jit(solution)/shard_map/all_to_all | solution.py:218
  107.2 19.9 %all_gather.3 = f32[8,192,128]{2,1,0:T(8,128)} all-gather(f32[1,192,128]{2,1,0:T(8,128)S(1)} %bitcast.10), channel_id=1, replica_groups=mesh['grp'=4,'far'=8,'near'=4,'core'=2] {'near','core'}, dimensions={0}, use_global_device_ids=true | all-gather | bytes 884736 | tf_op jit(solution)/shard_map/all_gather | solution.py:219
  127.1 13.8 %finish.1 = (f32[1024,256]{1,0:T(8,128)}, f32[4,4]{1,0:T(4,128)}) custom-call(f32[4,2,192,128]{3,2,1,0:T(8,128)} %bitcast.8, f32[1024,512]{1,0:T(8,128)} %q_hbm.1, f32[4,64,1024]{2,1,0:T(8,128)} %bitcast.7), custom_call_target="tpu_custom_call" | custom-call | tf_op jit(solution)/shard_map/finish/pallas_call | solution.py:222
  (3 shorter events, 0.0 us)
Async XLA Ops:
  5.7 22.0 %collective-permute-start = (f32[768,128]{1,0:T(8,128)}, f32[768,128]{1,0:T(8,128)S(1)}, u32[]{:S(2)}, u32[]{:S(2)}) collective-permute-start(f32[768,128]{1,0:T(8,128)} %get-tuple-element.5), channel_id=1, source_target_pairs={{0,1},{1,0},{2,3},{3,2},{4,5},{5,4},{6,7},{7,6},{8,9},{9,8},{10,11... | collective-permute-start | bytes 1179656 | tf_op jit(solution)/shard_map/ppermute | solution.py:213

commit v3 on v2

v3 whole, which is shorter than its diff:
```python
import functools

import jax
import jax.numpy as jnp
from jax import lax
from jax.experimental import pallas as pl
from jax.experimental.pallas import tpu as pltpu
from jax.sharding import Mesh
from jax.sharding import PartitionSpec as P

LEAF = 256
LANES = 128
NEAR = 4
CORES = 2
PIECES = 5
ROW = ("far", "near", "core")
GRP_ROW = ("grp",) + ROW
CHIP = ("far", "near")
SWAP = [(0, 1), (1, 0)]
NT = (((1,), (1,)), ((), ()))
TN = (((0,), (0,)), ((), ()))
NN = (((1,), (0,)), ((), ()))


def split(x):
    high = x.astype(jnp.bfloat16)
    low = (x - high.astype(jnp.float32)).astype(jnp.bfloat16)
    return high, low


def dot3(a, b, dims):
    dot = functools.partial(lax.dot_general, dimension_numbers=dims, preferred_element_type=jnp.float32)
    return dot(a[0], b[0]) + (dot(a[0], b[1]) + dot(a[1], b[0]))


def dot_full(a, b, dims):
    return lax.dot_general(a, b, dims, precision=lax.Precision.HIGHEST, preferred_element_type=jnp.float32)


def stats_kernel(core_ref, near_ref, q_ref, yt_ref, mine_ref, theirs_ref, acc_ref):
    step = pl.program_id(0)
    yt = yt_ref[...].reshape(-1, yt_ref.shape[2])
    basis = q_ref.shape[1]
    half = yt.shape[0] // CORES
    quarter = acc_ref.shape[1] // NEAR
    ys = split(yt)
    with_basis = dot3(ys, split(q_ref[...]), NN)
    with_self = dot3(ys, ys, NT) + lax.dot_general(ys[1], ys[1], NT, preferred_element_type=jnp.float32)

    @pl.when(step == 0)
    def _():
        acc_ref[...] = jnp.zeros_like(acc_ref)

    for c in range(CORES):
        rows = slice(c * half, (c + 1) * half)
        for product, base in ((with_basis, 0), (with_self, basis // LANES)):
            for block in range(product.shape[1] // LANES):
                at = (base + block) * half
                acc_ref[c, at:at + half, :] += product[rows, block * LANES:(block + 1) * LANES]

    @pl.when(step == pl.num_programs(0) - 1)
    def _():
        core = core_ref[0]
        for slot in range(NEAR):
            source = pl.multiple_of(lax.rem(near_ref[0] + slot, NEAR) * quarter, 8)
            rows = slice(slot * quarter, (slot + 1) * quarter)
            mine_ref[rows, :] = acc_ref[core, pl.ds(source, quarter), :]
            theirs_ref[rows, :] = acc_ref[1 - core, pl.ds(source, quarter), :]


def piece_rows(quarter):
    return ((0, 0, quarter), (1, 0, quarter), (3, 0, quarter), (2, 0, quarter // 2), (2, quarter // 2, quarter // 2))


def spread_row(x, r):
    return jnp.broadcast_to(x[r:r + 1], x.shape)


def factor_block(block, panel=16):
    size = block.shape[0]
    row_at = lax.broadcasted_iota(jnp.int32, (size, size), 0)
    lane_at = lax.broadcasted_iota(jnp.int32, (size, size), 1)
    eye = (row_at == lane_at).astype(jnp.float32)
    work = jnp.concatenate([block, eye], axis=1)
    width = 2 * size
    count = size // 8
    high = panel // 8
    parts = [work[8 * i:8 * i + 8] for i in range(count)]
    sub = lax.broadcasted_iota(jnp.int32, (8, width), 0)
    done = []
    for p in range(0, count, high):
        cols = {
            i: [jnp.take_along_axis(parts[i], jnp.full((8, width), 8 * p + m, jnp.int32), axis=1) for m in range(panel)]
            for i in range(p, count)
        }
        steps = []
        for q in range(p, p + high):
            pivots = None
            for r in range(8):
                m = 8 * (q - p) + r
                pivot = spread_row(cols[q][m], r)
                pivots = pivot if r == 0 else jnp.where(sub == r, pivot, pivots)
                inverse = 1.0 / pivot
                row = spread_row(parts[q], r)
                heads = {k: spread_row(cols[q][k], r) for k in range(m + 1, panel)}
                for i in range(q, p + high):
                    col = jnp.where(sub > r, cols[i][m], 0.0) if i == q else cols[i][m]
                    for k in range(m + 1, panel):
                        cols[i][k] = cols[i][k] - (col * heads[k]) * inverse
                    parts[i] = parts[i] - (col * row) * inverse
                steps.append((row * inverse, {k: heads[k] * inverse for k in heads}))
            done.append(parts[q] * lax.rsqrt(pivots))
        for i in range(p + high, count):
            col = cols[i]
            for m, (row, entries) in enumerate(steps):
                parts[i] = parts[i] - col[m] * row
                for k in range(m + 1, panel):
                    col[k] = col[k] - col[m] * entries[k]
    done = jnp.concatenate(done, axis=0)
    upper = jnp.where(row_at <= lane_at, done[:, :size], 0.0)
    return upper, done[:, size:]


def finish_kernel(leaves, core_ref, near_ref, *refs):
    parts = refs[:CORES * PIECES]
    q_hbm, yt_hbm, v_ref, est_ref, q_ref, yt_ref, work_ref, p_ref, sums_ref, sems = refs[CORES * PIECES:]
    q_copy = pltpu.make_async_copy(q_hbm, q_ref, sems.at[0])
    y_copy = pltpu.make_async_copy(yt_hbm, yt_ref, sems.at[1])
    q_copy.start()
    y_copy.start()
    rows, basis = q_ref.shape
    columns = yt_ref.shape[0] * yt_ref.shape[1]
    rounds = est_ref.shape[0]
    size = columns // rounds
    half = columns // CORES

    quarter = sums_ref.shape[1] // NEAR
    core, near = core_ref[0], near_ref[0]
    for side in range(CORES):
        half_at = core if side == 0 else 1 - core
        for piece, (slot, first, size_at) in enumerate(piece_rows(quarter)):
            at = pl.multiple_of(lax.rem(near + slot, NEAR) * quarter + first, 8)
            sums_ref[half_at, pl.ds(at, size_at), :] = parts[side * PIECES + piece][...]

    def lanes_block(block):
        return jnp.concatenate([sums_ref[c, block * half:(block + 1) * half, :] for c in range(CORES)], axis=0)

    coefs = jnp.concatenate([lanes_block(b) for b in range(basis // LANES)], axis=1)
    own = jnp.concatenate([lanes_block(basis // LANES + b) for b in range(columns // LANES)], axis=1)
    row_at = lax.broadcasted_iota(jnp.int32, (columns, columns), 0)
    lane_at = lax.broadcasted_iota(jnp.int32, (columns, columns), 1)
    work_ref[:, :columns] = own - dot_full(coefs, coefs, NT)
    work_ref[:, columns:] = (row_at == lane_at).astype(jnp.float32)
    coefs_s = split(coefs)
    leaf_count = rows // LEAF

    def project(leaf):
        span = slice(leaf * LEAF, (leaf + 1) * LEAF)
        block = yt_ref[:, :, span].reshape(columns, LEAF).T
        p_ref[span, :] = block - dot3(split(q_ref[span, :]), coefs_s, NT)

    uppers = []
    for k in range(rounds):
        here = slice(k * size, (k + 1) * size)
        after = slice((k + 1) * size, columns)
        if k > 0:
            for leaf in range((k - 1) * leaf_count // (rounds - 1), k * leaf_count // (rounds - 1)):
                project(leaf)
        upper, inverse = factor_block(work_ref[here, here])
        uppers.append(upper)
        done = dot_full(inverse, work_ref[here, :], NN)
        work_ref[here, :] = done
        if k + 1 < rounds:
            work_ref[after, :] -= dot_full(done[:, after], done, TN)
        if k == 0:
            q_copy.wait()
            y_copy.wait()
    zero = jnp.zeros((size, size), jnp.float32)
    diagonal = jnp.concatenate(
        [jnp.concatenate([uppers[k] if j == k else zero for j in range(rounds)], axis=1) for k in range(rounds)], axis=0
    )
    inverse = work_ref[:, columns:]
    inverse_t = split(jnp.where(row_at >= lane_at, inverse, 0.0))
    diagonal_s = split(diagonal)
    sums = []
    for leaf in range(leaf_count):
        span = slice(leaf * LEAF, (leaf + 1) * LEAF)
        fresh = dot3(split(p_ref[span, :]), inverse_t, NT)
        v_ref[span, :] = fresh
        remainder = dot3(split(fresh), diagonal_s, NN)
        sums.append(jnp.sum(remainder * remainder, axis=0, keepdims=True))
    count = len(sums)
    member = (
        lax.broadcasted_iota(jnp.int32, (8, columns), 0)
        == lax.broadcasted_iota(jnp.int32, (8, columns), 1) // size
    ).astype(jnp.float32)
    leaf_energy = dot_full(member, jnp.concatenate(sums + [jnp.zeros((8 - count, columns), jnp.float32)], axis=0), NT)
    energies = jnp.sum(jnp.where(row_at == lane_at, own, 0.0), axis=0, keepdims=True)
    energy = jnp.sum(member * energies, axis=1, keepdims=True)
    est_ref[...] = jnp.sqrt(leaves * leaf_energy / energy)[:rounds, :count]


def run_finish(leaves, core, near, parts, prior_basis, samples_t):
    rows, basis = prior_basis.shape
    rounds, size, _ = samples_t.shape
    columns = rounds * size
    depth = (basis + columns) // LANES * (columns // CORES)
    whole = pl.BlockSpec(memory_space=pltpu.VMEM)
    return pl.pallas_call(
        functools.partial(finish_kernel, leaves),
        in_specs=[pl.BlockSpec(memory_space=pltpu.SMEM)] * 2
        + [whole] * len(parts)
        + [pl.BlockSpec(memory_space=pl.ANY), pl.BlockSpec(memory_space=pl.ANY)],
        out_specs=[whole, whole],
        out_shape=[
            jax.ShapeDtypeStruct((rows, columns), jnp.float32),
            jax.ShapeDtypeStruct((rounds, rows // LEAF), jnp.float32),
        ],
        scratch_shapes=[
            pltpu.VMEM((rows, basis), jnp.float32),
            pltpu.VMEM((rounds, size, rows), jnp.float32),
            pltpu.VMEM((columns, 2 * columns), jnp.float32),
            pltpu.VMEM((rows, columns), jnp.float32),
            pltpu.VMEM((CORES, depth, LANES), jnp.float32),
            pltpu.SemaphoreType.DMA((2,)),
        ],
        name="finish",
    )(core, near, *parts, prior_basis, samples_t)


def shifted(x, hops):
    count = lax.axis_size(CHIP)
    return lax.ppermute(x, CHIP, [(i, (i + hops) % count) for i in range(count)])


def local(prior_basis, samples):
    rounds, rows, size = samples.shape
    basis = prior_basis.shape[1]
    columns = rounds * size
    half = columns // CORES
    depth = (basis + columns) // LANES * half
    quarter = depth // NEAR
    far = lax.axis_size("far")
    core = lax.axis_index("core").reshape(1).astype(jnp.int32)
    near = lax.axis_index("near").reshape(1).astype(jnp.int32)
    step = LEAF
    samples_t = jnp.transpose(samples, (0, 2, 1))
    mine, theirs = pl.pallas_call(
        stats_kernel,
        grid=(rows // step,),
        in_specs=[
            pl.BlockSpec(memory_space=pltpu.SMEM),
            pl.BlockSpec(memory_space=pltpu.SMEM),
            pl.BlockSpec((step, basis), lambda i: (i, 0)),
            pl.BlockSpec((rounds, size, step), lambda i: (0, 0, i)),
        ],
        out_specs=[
            pl.BlockSpec((depth, LANES), lambda i: (0, 0)),
            pl.BlockSpec((depth, LANES), lambda i: (0, 0)),
        ],
        out_shape=[
            jax.ShapeDtypeStruct((depth, LANES), jnp.float32),
            jax.ShapeDtypeStruct((depth, LANES), jnp.float32),
        ],
        scratch_shapes=[pltpu.VMEM((CORES, depth, LANES), jnp.float32)],
        name="stats",
    )(core, near, prior_basis, samples_t)
    chip = (mine + lax.ppermute(theirs, "core", SWAP)).reshape(NEAR, quarter, LANES)
    middle = quarter // 2
    from_left = shifted(chip[1], 1)
    from_right = shifted(chip[3], -1)
    from_far_left = shifted(chip[2, :middle], 2)
    from_far_right = shifted(chip[2, middle:], -2)
    near_sum = chip[0] + from_left + from_right + jnp.concatenate([from_far_left, from_far_right], axis=0)
    far_parts = lax.all_to_all(near_sum.reshape(far, quarter // far, LANES), "far", 0, 0, tiled=True)
    total = jnp.sum(far_parts, axis=0)
    own = lax.all_to_all(jnp.broadcast_to(total, far_parts.shape), "far", 0, 0, tiled=True).reshape(quarter, LANES)
    pieces = [own, shifted(own, -1), shifted(own, 1), shifted(own[:middle], 2), shifted(own[middle:], -2)]
    parts = pieces + [lax.ppermute(piece, "core", SWAP) for piece in pieces]
    leaves = float(rows // LEAF * far * NEAR * CORES)
    return run_finish(leaves, core, near, parts, prior_basis, samples_t)


def solution(mesh):
    grp = mesh.shape["grp"]
    far = mesh.shape["row"] // (NEAR * CORES)
    parts = Mesh(mesh.devices.reshape(grp, far, NEAR, CORES), GRP_ROW)
    in_specs = (P(GRP_ROW, None), P(None, GRP_ROW, None))
    out_specs = (P(GRP_ROW, None), P(None, GRP_ROW))
    return jax.shard_map(local, mesh=parts, in_specs=in_specs, out_specs=out_specs, check_vma=False)
```

time: 141 us -> 131 us (0.929)
  blocking collectives: 98.3 us -> 62.2 us
  starting transfers between devices: 20.4 us -> 43.1 us
  waiting for transfers between devices: 1.56 us -> 4.34 us
    ppermute x1 -> x14, starting transfers between devices: 20.4 us -> 43.1 us  [the longest x1 20.4 us: local(): lax.ppermute(theirs, 'core', SWAP)]
    all_gather x1 -> x0, blocking collectives: 19.9 us -> none  [local(): lax.all_gather(far_all.reshape(1, depth // NEAR, LANES), ('near', 'core')...]
    all_to_all x2 -> x1, blocking collectives: 49.7 us -> 34.4 us  [local(): lax.all_to_all(near_sum.reshape(far, quarter // far, LANES), 'far', 0, 0,...]
    ppermute x1 -> x14, waiting for transfers between devices: 1.56 us -> 4.34 us  [the longest x8 1.86 us: shifted(): lax.ppermute(x, CHIP, [(i, (i + hops) % count) for i in range(count)])]
    pallas_call x1, Pallas kernels: 13.8 us -> 12.4 us  [run_finish(): pl.pallas_call(functools.partial(finish_kernel, leaves), in_specs=[pl.Blo...]
  transfers between devices with their start and end apart: 1 -> 14, of which waited for: 1 -> 5; matrix products, arithmetic and copies ran while one was open for 0% -> 0% of each run, Pallas kernels for 0% -> 0%
where the time goes in v3:
time: 131 us; the launch traced here: 130 us
  blocking collectives  62.2 us (47%)
  starting transfers between devices  43.1 us (33%)
  Pallas kernels  17.4 us (13%)
  waiting for transfers between devices  4.34 us (3%)
  local copies, waits for them, and re-layouts  1.31 us (1%)
    all_to_all x1, blocking collectives, local(): lax.all_to_all(near_sum.reshape(far, quarter // far, LANES), 'far', 0, 0,...  34.4 us
    all_to_all x1, blocking collectives, local(): lax.all_to_all(jnp.broadcast_to(total, far_parts.shape), 'far', 0, 0, til...  27.8 us
    ppermute x1, starting transfers between devices, local(): lax.ppermute(theirs, 'core', SWAP)  20.4 us
    ppermute x8, starting transfers between devices, shifted(): lax.ppermute(x, CHIP, [(i, (i + hops) % count) for i in range(count)])  14 us
    pallas_call x1, Pallas kernels, run_finish(): pl.pallas_call(functools.partial(finish_kernel, leaves), in_specs=[pl.Blo...  12.4 us
    ppermute x5, starting transfers between devices, local(): parts = pieces + [lax.ppermute(piece, 'core', SWAP) for piece in pieces]  8.61 us
    pallas_call x1, Pallas kernels, local(): pl.pallas_call(stats_kernel, grid=(rows // step,), in_specs=[pl.BlockSpec...  5.06 us
  transfers between devices with their start and end apart: 14, of which 5 were waited for; matrix products, arithmetic and copies ran while one was open for 0% of the time, Pallas kernels for 0%

profile of v3, /device:TPU:37, one launch (start us, length us, event | category | flops | bytes accessed | tf_op | source)
XLA Modules:
  0.0 130.3 jit_solution(9737142823840819648)
XLA Ops:
  0.6 5.1 %stats.1 = (f32[768,128]{1,0:T(8,128)}, f32[768,128]{1,0:T(8,128)}) custom-call(s32[1]{0:T(128)} %bitcast.core_ref, s32[1]{0:T(128)} %bitcast.1.near_ref, f32[1024,512]{1,0:T(8,128)} %refs_10_.1, f32[4,64,1024]{2,1,0:T(8,128)} %bitcast.12), custom_call_target="tpu_custom_call" | custom-call | tf_op jit(solution)/shard_map/stats/pallas_call | solution.py:248
  5.7 20.4 %collective-permute-start = (f32[768,128]{1,0:T(8,128)}, f32[768,128]{1,0:T(8,128)S(1)}, u32[]{:S(2)}, u32[]{:S(2)}) collective-permute-start(f32[768,128]{1,0:T(8,128)} %get-tuple-element.5), channel_id=1, source_target_pairs={{0,1},{1,0},{2,3},{3,2},{4,5},{5,4},{6,7},{7,6},{8,9},{9,8},{10,11... | collective-permute-start | bytes 1179656 | tf_op jit(solution)/shard_map/ppermute | solution.py:268
  26.1 1.6 %collective-permute-done = f32[768,128]{1,0:T(8,128)S(1)} collective-permute-done((f32[768,128]{1,0:T(8,128)}, f32[768,128]{1,0:T(8,128)S(1)}, u32[]{:S(2)}, u32[]{:S(2)}) %collective-permute-start) | collective-permute-done | bytes 393248 | tf_op jit(solution)/shard_map/ppermute | solution.py:268
  27.7 1.1 add.12
  28.7 0.1 collective-permute-start.1
  28.9 3.9 %collective-permute-start.2 = (f32[192,128]{1,0:T(8,128)S(1)}, f32[192,128]{1,0:T(8,128)S(1)}, u32[]{:S(2)}, u32[]{:S(2)}) collective-permute-start(f32[192,128]{1,0:T(8,128)S(1)} %get-tuple-element.9), channel_id=1, source_target_pairs={{0,62},{2,0},{4,2},{6,4},{8,6},{10,8},{12,10},{14,12},{16,14},{18,... | collective-permute-start | bytes 294920 | tf_op jit(solution)/shard_map/ppermute | solution.py:233
  32.8 0.1 collective-permute-start.3
  32.9 3.5 %collective-permute-start.4 = (f32[96,128]{1,0:T(8,128)S(1)}, f32[96,128]{1,0:T(8,128)S(1)}, u32[]{:S(2)}, u32[]{:S(2)}) collective-permute-start(f32[96,128]{1,0:T(8,128)S(1)} %get-tuple-element.7), channel_id=1, source_target_pairs={{0,60},{2,62},{4,0},{6,2},{8,4},{10,6},{12,8},{14,10},{16,12},{18,... | collective-permute-start | bytes 147464 | tf_op jit(solution)/shard_map/ppermute | solution.py:233
  36.5 1.6 %collective-permute-done.3 = f32[96,128]{1,0:T(8,128)S(1)} collective-permute-done((f32[96,128]{1,0:T(8,128)S(1)}, f32[96,128]{1,0:T(8,128)S(1)}, u32[]{:S(2)}, u32[]{:S(2)}) %collective-permute-start.3) | collective-permute-done | bytes 49184 | tf_op jit(solution)/shard_map/ppermute | solution.py:233
  38.1 0.0 collective-permute-done.4
  38.1 0.0 collective-permute-done.1
  38.1 0.0 collective-permute-done.2
  38.1 34.4 %all_to_all.10 = f32[8,24,128]{2,1,0:T(8,128)S(1)} all-to-all(f32[8,24,128]{2,1,0:T(8,128)S(1)} %bitcast.19), channel_id=1, replica_groups=mesh['grp'=4,'far'=8,'near'=4,'core'=2] {'far'}, dimensions={0} | all-to-all | bytes 196608 | tf_op jit(solution)/shard_map/all_to_all | solution.py:275
  72.6 27.8 %all_to_all.11 = f32[8,24,128]{2,1,0:T(8,128)S(1)} all-to-all(f32[8,24,128]{2,1,0:T(8,128)S(1)} %broadcast_in_dim.3), channel_id=1, replica_groups=mesh['grp'=4,'far'=8,'near'=4,'core'=2] {'far'}, dimensions={0} | all-to-all | bytes 196608 | tf_op jit(solution)/shard_map/all_to_all | solution.py:277
  100.4 0.0 copy-start
  100.4 5.3 %collective-permute-start.9 = (f32[192,128]{1,0:T(8,128)S(1)}, f32[192,128]{1,0:T(8,128)S(1)}, u32[]{:S(2)}, u32[]{:S(2)}) collective-permute-start(f32[192,128]{1,0:T(8,128)S(1)} %bitcast.15), channel_id=1, source_target_pairs={{0,1},{1,0},{2,3},{3,2},{4,5},{5,4},{6,7},{7,6},{8,9},{9,8},{10,11... | collective-permute-start | bytes 294920 | tf_op jit(solution)/shard_map/ppermute | solution.py:279
  105.7 0.4 collective-permute-start.6
  106.1 2.3 %collective-permute-start.5 = (f32[192,128]{1,0:T(8,128)S(1)}, f32[192,128]{1,0:T(8,128)S(1)}, u32[]{:S(2)}, u32[]{:S(2)}) collective-permute-start(f32[192,128]{1,0:T(8,128)S(1)} %bitcast.17), channel_id=1, source_target_pairs={{0,62},{2,0},{4,2},{6,4},{8,6},{10,8},{12,10},{14,12},{16,14},{18,... | collective-permute-start | bytes 294920 | tf_op jit(solution)/shard_map/ppermute | solution.py:233
  108.4 0.6 collective-permute-start.7
  109.0 3.0 %collective-permute-start.8 = (f32[96,128]{1,0:T(8,128)S(1)}, f32[96,128]{1,0:T(8,128)S(1)}, u32[]{:S(2)}, u32[]{:S(2)}) collective-permute-start(f32[96,128]{1,0:T(8,128)S(1)} %bitcast.20), channel_id=1, source_target_pairs={{0,60},{2,62},{4,0},{6,2},{8,4},{10,6},{12,8},{14,10},{16,12},{18,... | collective-permute-start | bytes 147464 | tf_op jit(solution)/shard_map/ppermute | solution.py:233
  112.1 0.0 collective-permute-done.6.refs_2_
  112.1 0.0 copy-start.2
  112.1 1.1 collective-permute-start.11
  113.2 0.0 collective-permute-done.5.refs_1_
  113.2 0.0 copy-start.3
  113.2 0.1 collective-permute-start.10
  113.3 0.2 collective-permute-done.7.refs_3_
  113.5 0.0 copy-start.6
  113.5 1.7 %collective-permute-start.12 = (f32[96,128]{1,0:T(8,128)S(1)}, f32[96,128]{1,0:T(8,128)S(1)}, u32[]{:S(2)}, u32[]{:S(2)}) collective-permute-start(f32[96,128]{1,0:T(8,128)S(1)} %collective-permute-done.7.refs_3_), channel_id=1, source_target_pairs={{0,1},{1,0},{2,3},{3,2},{4,5},{5,4},{6,7},{7,6},{8,9},{9,8},{10,11... | collective-permute-start | bytes 147464 | tf_op jit(solution)/shard_map/ppermute | solution.py:279
  115.3 0.0 collective-permute-done.8.refs_4_
  115.3 0.0 copy-start.7
  115.3 0.3 collective-permute-start.13
  115.6 0.6 collective-permute-done.12.refs_8_
  116.1 0.0 copy-start.8
  116.1 0.4 collective-permute-done.13.refs_9_
  116.5 0.0 copy-start.9
  116.5 0.0 collective-permute-done.9.refs_5_
  116.5 0.0 copy-start.1
  116.5 0.0 collective-permute-done.11.refs_7_
  116.5 0.0 copy-start.4
  116.5 0.0 collective-permute-done.10.refs_6_
  116.5 0.0 copy-done
  116.5 0.0 copy-done.2
  116.5 0.0 copy-done.3
  116.6 0.0 copy-done.6
  116.6 0.0 copy-done.7
  116.6 0.2 copy-done.8
  116.7 0.4 copy-done.9
  117.1 0.0 copy-done.1
  117.2 0.0 copy-done.4
  117.2 0.0 copy-start.5
  117.2 0.6 copy-done.5
  117.8 12.4 %finish.1 = (f32[1024,256]{1,0:T(8,128)}, f32[4,4]{1,0:T(4,128)}) custom-call(s32[1]{0:T(128)} %bitcast.core_ref, s32[1]{0:T(128)} %bitcast.1.near_ref, f32[192,128]{1,0:T(8,128)} %bitcast.18, f32[192,128]{1,0:T(8,128)} %copy-done.3, f32[192,128]{1,0:T(8,128)} %copy-done.2, f32[96,128]{1,0:T(8,128)} %copy-done.6, f32[96,128]{1,0:T(8,128)} %copy-done.7, ...), custom_call_target="tpu_custom_call" | custom-call | tf_op jit(solution)/shard_map/finish/pallas_call | solution.py:209
  (6 shorter events, 0.1 us)
Async XLA Ops:
  5.7 22.0 %collective-permute-start = (f32[768,128]{1,0:T(8,128)}, f32[768,128]{1,0:T(8,128)S(1)}, u32[]{:S(2)}, u32[]{:S(2)}) collective-permute-start(f32[768,128]{1,0:T(8,128)} %get-tuple-element.5), channel_id=1, source_target_pairs={{0,1},{1,0},{2,3},{3,2},{4,5},{5,4},{6,7},{7,6},{8,9},{9,8},{10,11... | collective-permute-start | bytes 1179656 | tf_op jit(solution)/shard_map/ppermute | solution.py:268
  28.7 9.4 %collective-permute-start.1 = (f32[192,128]{1,0:T(8,128)S(1)}, f32[192,128]{1,0:T(8,128)S(1)}, u32[]{:S(2)}, u32[]{:S(2)}) collective-permute-start(f32[192,128]{1,0:T(8,128)S(1)} %get-tuple-element.8), channel_id=1, source_target_pairs={{0,2},{2,4},{4,6},{6,8},{8,10},{10,12},{12,14},{14,16},{16,18},{18... | collective-permute-start | bytes 294920 | tf_op jit(solution)/shard_map/ppermute | solution.py:233
  28.9 9.2 %collective-permute-start.2 = (f32[192,128]{1,0:T(8,128)S(1)}, f32[192,128]{1,0:T(8,128)S(1)}, u32[]{:S(2)}, u32[]{:S(2)}) collective-permute-start(f32[192,128]{1,0:T(8,128)S(1)} %get-tuple-element.9), channel_id=1, source_target_pairs={{0,62},{2,0},{4,2},{6,4},{8,6},{10,8},{12,10},{14,12},{16,14},{18,... | collective-permute-start | bytes 294920 | tf_op jit(solution)/shard_map/ppermute | solution.py:233
  32.8 5.3 %collective-permute-start.3 = (f32[96,128]{1,0:T(8,128)S(1)}, f32[96,128]{1,0:T(8,128)S(1)}, u32[]{:S(2)}, u32[]{:S(2)}) collective-permute-start(f32[96,128]{1,0:T(8,128)S(1)} %get-tuple-element.6), channel_id=1, source_target_pairs={{0,4},{2,6},{4,8},{6,10},{8,12},{10,14},{12,16},{14,18},{16,20},{1... | collective-permute-start | bytes 147464 | tf_op jit(solution)/shard_map/ppermute | solution.py:233
  32.9 5.2 %collective-permute-start.4 = (f32[96,128]{1,0:T(8,128)S(1)}, f32[96,128]{1,0:T(8,128)S(1)}, u32[]{:S(2)}, u32[]{:S(2)}) collective-permute-start(f32[96,128]{1,0:T(8,128)S(1)} %get-tuple-element.7), channel_id=1, source_target_pairs={{0,60},{2,62},{4,0},{6,2},{8,4},{10,6},{12,8},{14,10},{16,12},{18,... | collective-permute-start | bytes 147464 | tf_op jit(solution)/shard_map/ppermute | solution.py:233
  100.4 16.1 %copy-start = (f32[8,24,128]{2,1,0:T(8,128)}, f32[8,24,128]{2,1,0:T(8,128)S(1)}, u32[]{:S(2)}) copy-start(f32[8,24,128]{2,1,0:T(8,128)S(1)} %all_to_all.11) | copy-start | bytes 294916
  100.4 16.1 %collective-permute-start.9 = (f32[192,128]{1,0:T(8,128)S(1)}, f32[192,128]{1,0:T(8,128)S(1)}, u32[]{:S(2)}, u32[]{:S(2)}) collective-permute-start(f32[192,128]{1,0:T(8,128)S(1)} %bitcast.15), channel_id=1, source_target_pairs={{0,1},{1,0},{2,3},{3,2},{4,5},{5,4},{6,7},{7,6},{8,9},{9,8},{10,11... | collective-permute-start | bytes 294920 | tf_op jit(solution)/shard_map/ppermute | solution.py:279
  105.7 6.4 %collective-permute-start.6 = (f32[192,128]{1,0:T(8,128)S(1)}, f32[192,128]{1,0:T(8,128)S(1)}, u32[]{:S(2)}, u32[]{:S(2)}) collective-permute-start(f32[192,128]{1,0:T(8,128)S(1)} %bitcast.16), channel_id=1, source_target_pairs={{0,2},{2,4},{4,6},{6,8},{8,10},{10,12},{12,14},{14,16},{16,18},{18... | collective-permute-start | bytes 294920 | tf_op jit(solution)/shard_map/ppermute | solution.py:233
  106.1 7.1 %collective-permute-start.5 = (f32[192,128]{1,0:T(8,128)S(1)}, f32[192,128]{1,0:T(8,128)S(1)}, u32[]{:S(2)}, u32[]{:S(2)}) collective-permute-start(f32[192,128]{1,0:T(8,128)S(1)} %bitcast.17), channel_id=1, source_target_pairs={{0,62},{2,0},{4,2},{6,4},{8,6},{10,8},{12,10},{14,12},{16,14},{18,... | collective-permute-start | bytes 294920 | tf_op jit(solution)/shard_map/ppermute | solution.py:233
  108.4 5.2 %collective-permute-start.7 = (f32[96,128]{1,0:T(8,128)S(1)}, f32[96,128]{1,0:T(8,128)S(1)}, u32[]{:S(2)}, u32[]{:S(2)}) collective-permute-start(f32[96,128]{1,0:T(8,128)S(1)} %bitcast.21), channel_id=1, source_target_pairs={{0,4},{2,6},{4,8},{6,10},{8,12},{10,14},{12,16},{14,18},{16,20},{1... | collective-permute-start | bytes 147464 | tf_op jit(solution)/shard_map/ppermute | solution.py:233
  109.0 6.2 %collective-permute-start.8 = (f32[96,128]{1,0:T(8,128)S(1)}, f32[96,128]{1,0:T(8,128)S(1)}, u32[]{:S(2)}, u32[]{:S(2)}) collective-permute-start(f32[96,128]{1,0:T(8,128)S(1)} %bitcast.20), channel_id=1, source_target_pairs={{0,60},{2,62},{4,0},{6,2},{8,4},{10,6},{12,8},{14,10},{16,12},{18,... | collective-permute-start | bytes 147464 | tf_op jit(solution)/shard_map/ppermute | solution.py:233
  112.1 4.5 %copy-start.2 = (f32[192,128]{1,0:T(8,128)}, f32[192,128]{1,0:T(8,128)S(1)}, u32[]{:S(2)}) copy-start(f32[192,128]{1,0:T(8,128)S(1)} %collective-permute-done.6.refs_2_) | copy-start | bytes 294916
  112.1 4.4 %collective-permute-start.11 = (f32[192,128]{1,0:T(8,128)S(1)}, f32[192,128]{1,0:T(8,128)S(1)}, u32[]{:S(2)}, u32[]{:S(2)}) collective-permute-start(f32[192,128]{1,0:T(8,128)S(1)} %collective-permute-done.6.refs_2_), channel_id=1, source_target_pairs={{0,1},{1,0},{2,3},{3,2},{4,5},{5,4},{6,7},{7,6},{8,9},{9,8},{10,11... | collective-permute-start | bytes 294920 | tf_op jit(solution)/shard_map/ppermute | solution.py:279
  113.2 3.4 %copy-start.3 = (f32[192,128]{1,0:T(8,128)}, f32[192,128]{1,0:T(8,128)S(1)}, u32[]{:S(2)}) copy-start(f32[192,128]{1,0:T(8,128)S(1)} %collective-permute-done.5.refs_1_) | copy-start | bytes 294916
  113.2 3.3 %collective-permute-start.10 = (f32[192,128]{1,0:T(8,128)S(1)}, f32[192,128]{1,0:T(8,128)S(1)}, u32[]{:S(2)}, u32[]{:S(2)}) collective-permute-start(f32[192,128]{1,0:T(8,128)S(1)} %collective-permute-done.5.refs_1_), channel_id=1, source_target_pairs={{0,1},{1,0},{2,3},{3,2},{4,5},{5,4},{6,7},{7,6},{8,9},{9,8},{10,11... | collective-permute-start | bytes 294920 | tf_op jit(solution)/shard_map/ppermute | solution.py:279
  113.5 3.0 %copy-start.6 = (f32[96,128]{1,0:T(8,128)}, f32[96,128]{1,0:T(8,128)S(1)}, u32[]{:S(2)}) copy-start(f32[96,128]{1,0:T(8,128)S(1)} %collective-permute-done.7.refs_3_) | copy-start | bytes 147460
  113.5 2.6 %collective-permute-start.12 = (f32[96,128]{1,0:T(8,128)S(1)}, f32[96,128]{1,0:T(8,128)S(1)}, u32[]{:S(2)}, u32[]{:S(2)}) collective-permute-start(f32[96,128]{1,0:T(8,128)S(1)} %collective-permute-done.7.refs_3_), channel_id=1, source_target_pairs={{0,1},{1,0},{2,3},{3,2},{4,5},{5,4},{6,7},{7,6},{8,9},{9,8},{10,11... | collective-permute-start | bytes 147464 | tf_op jit(solution)/shard_map/ppermute | solution.py:279
  115.3 1.3 %copy-start.7 = (f32[96,128]{1,0:T(8,128)}, f32[96,128]{1,0:T(8,128)S(1)}, u32[]{:S(2)}) copy-start(f32[96,128]{1,0:T(8,128)S(1)} %collective-permute-done.8.refs_4_) | copy-start | bytes 147460
  115.3 1.2 collective-permute-start.13
  116.1 0.6 copy-start.8
  116.5 0.6 copy-start.9
  116.5 0.7 copy-start.1
  116.5 0.7 copy-start.4
  117.2 0.6 copy-start.5

commit v4 on v3

--- a/solution.py
+++ b/solution.py
@@ -28,13 +28,19 @@
     return high, low
 
 
+def dot_parts(a, b, dims, pairs):
+    ((lhs_at,), (rhs_at,)), _ = dims
+    lhs = jnp.concatenate([a[i] for i, _ in pairs], axis=lhs_at)
+    rhs = jnp.concatenate([b[j] for _, j in pairs], axis=rhs_at)
+    return lax.dot_general(lhs, rhs, dims, preferred_element_type=jnp.float32)
+
+
 def dot3(a, b, dims):
-    dot = functools.partial(lax.dot_general, dimension_numbers=dims, preferred_element_type=jnp.float32)
-    return dot(a[0], b[0]) + (dot(a[0], b[1]) + dot(a[1], b[0]))
-
-
-def dot_full(a, b, dims):
-    return lax.dot_general(a, b, dims, precision=lax.Precision.HIGHEST, preferred_element_type=jnp.float32)
+    return dot_parts(a, b, dims, ((0, 0), (0, 1), (1, 0)))
+
+
+def dot4(a, b, dims):
+    return dot_parts(a, b, dims, ((0, 0), (0, 1), (1, 0), (1, 1)))
 
 
 def stats_kernel(core_ref, near_ref, q_ref, yt_ref, mine_ref, theirs_ref, acc_ref):
@@ -45,7 +51,7 @@
     quarter = acc_ref.shape[1] // NEAR
     ys = split(yt)
     with_basis = dot3(ys, split(q_ref[...]), NN)
-    with_self = dot3(ys, ys, NT) + lax.dot_general(ys[1], ys[1], NT, preferred_element_type=jnp.float32)
+    with_self = dot4(ys, ys, NT)
 
     @pl.when(step == 0)
     def _():
@@ -149,7 +155,9 @@
     own = jnp.concatenate([lanes_block(basis // LANES + b) for b in range(columns // LANES)], axis=1)
     row_at = lax.broadcasted_iota(jnp.int32, (columns, columns), 0)
     lane_at = lax.broadcasted_iota(jnp.int32, (columns, columns), 1)
-    work_ref[:, :columns] = own - dot_full(coefs, coefs, NT)
+    work_ref[:, :columns] = own - lax.dot_general(
+        coefs, coefs, NT, precision=lax.Precision.HIGHEST, preferred_element_type=jnp.float32
+    )
     work_ref[:, columns:] = (row_at == lane_at).astype(jnp.float32)
     coefs_s = split(coefs)
     leaf_count = rows // LEAF
@@ -168,10 +176,10 @@
                 project(leaf)
         upper, inverse = factor_block(work_ref[here, here])
         uppers.append(upper)
-        done = dot_full(inverse, work_ref[here, :], NN)
+        done = dot4(split(inverse), split(work_ref[here, :]), NN)
         work_ref[here, :] = done
         if k + 1 < rounds:
-            work_ref[after, :] -= dot_full(done[:, after], done, TN)
+            work_ref[after, :] -= dot4(split(done[:, after]), split(done), TN)
         if k == 0:
             q_copy.wait()
             y_copy.wait()
@@ -194,7 +202,8 @@
         lax.broadcasted_iota(jnp.int32, (8, columns), 0)
         == lax.broadcasted_iota(jnp.int32, (8, columns), 1) // size
     ).astype(jnp.float32)
-    leaf_energy = dot_full(member, jnp.concatenate(sums + [jnp.zeros((8 - count, columns), jnp.float32)], axis=0), NT)
+    leaf_sums = jnp.concatenate(sums + [jnp.zeros((8 - count, columns), jnp.float32)], axis=0)
+    leaf_energy = dot4(split(member), split(leaf_sums), NT)
     energies = jnp.sum(jnp.where(row_at == lane_at, own, 0.0), axis=0, keepdims=True)
     energy = jnp.sum(member * energies, axis=1, keepdims=True)
     est_ref[...] = jnp.sqrt(leaves * leaf_energy / energy)[:rounds, :count]
@@ -206,6 +215,7 @@
     columns = rounds * size
     depth = (basis + columns) // LANES * (columns // CORES)
     whole = pl.BlockSpec(memory_space=pltpu.VMEM)
+    held = [pltpu.with_memory_space_constraint(part, pltpu.VMEM) for part in parts]
     return pl.pallas_call(
         functools.partial(finish_kernel, leaves),
         in_specs=[pl.BlockSpec(memory_space=pltpu.SMEM)] * 2
@@ -225,7 +235,7 @@
             pltpu.SemaphoreType.DMA((2,)),
         ],
         name="finish",
-    )(core, near, *parts, prior_basis, samples_t)
+    )(core, near, *held, prior_basis, samples_t)
 
 
 def shifted(x, hops):
@@ -255,13 +265,10 @@
             pl.BlockSpec((rounds, size, step), lambda i: (0, 0, i)),
         ],
         out_specs=[
-            pl.BlockSpec((depth, LANES), lambda i: (0, 0)),
-            pl.BlockSpec((depth, LANES), lambda i: (0, 0)),
-        ],
-        out_shape=[
-            jax.ShapeDtypeStruct((depth, LANES), jnp.float32),
-            jax.ShapeDtypeStruct((depth, LANES), jnp.float32),
-        ],
+            pl.BlockSpec(memory_space=pltpu.VMEM),
+            pl.BlockSpec(memory_space=pltpu.VMEM),
+        ],
+        out_shape=[pltpu.VMEM((depth, LANES), jnp.float32), pltpu.VMEM((depth, LANES), jnp.float32)],
         scratch_shapes=[pltpu.VMEM((CORES, depth, LANES), jnp.float32)],
         name="stats",
     )(core, near, prior_basis, samples_t)

time: 131 us -> 125 us (0.954)
  Pallas kernels: 17.4 us -> 14.3 us
    pallas_call x1, Pallas kernels: 12.4 us -> 10.1 us  [run_finish(): pl.pallas_call(functools.partial(finish_kernel, leaves), in_specs=[pl.Blo...]
where the time goes in v4:
time: 125 us
  blocking collectives  62.2 us (50%)
  starting transfers between devices  42.9 us (34%)
  Pallas kernels  14.3 us (11%)
  waiting for transfers between devices  4.46 us (4%)
    all_to_all x1, blocking collectives, local(): lax.all_to_all(near_sum.reshape(far, quarter // far, LANES), 'far', 0, 0,...  34.4 us
    all_to_all x1, blocking collectives, local(): lax.all_to_all(jnp.broadcast_to(total, far_parts.shape), 'far', 0, 0, til...  27.8 us
    ppermute x1, starting transfers between devices, local(): lax.ppermute(theirs, 'core', SWAP)  20.5 us
    ppermute x8, starting transfers between devices, shifted(): lax.ppermute(x, CHIP, [(i, (i + hops) % count) for i in range(count)])  14 us
    pallas_call x1, Pallas kernels, run_finish(): pl.pallas_call(functools.partial(finish_kernel, leaves), in_specs=[pl.Blo...  10.1 us
    ppermute x5, starting transfers between devices, local(): parts = pieces + [lax.ppermute(piece, 'core', SWAP) for piece in pieces]  8.3 us
    pallas_call x1, Pallas kernels, local(): pl.pallas_call(stats_kernel, grid=(rows // step,), in_specs=[pl.BlockSpec...  4.2 us
  transfers between devices with their start and end apart: 14, of which 5 were waited for; matrix products, arithmetic and copies ran while one was open for 0% of the time, Pallas kernels for 0%

profile of v4, /device:TPU:37, one launch (start us, length us, event | category | flops | bytes accessed | tf_op | source)
XLA Modules:
  0.0 124.8 jit_solution(11226647430616691928)
XLA Ops:
  0.6 4.2 %stats.1 = (f32[768,128]{1,0:T(8,128)S(1)}, f32[768,128]{1,0:T(8,128)S(1)}) custom-call(s32[1]{0:T(128)} %bitcast.core_ref, s32[1]{0:T(128)} %bitcast.1.near_ref, f32[1024,512]{1,0:T(8,128)} %refs_10_.1, f32[4,64,1024]{2,1,0:T(8,128)} %bitcast.16), custom_call_target="tpu_custom_call" | custom-call | tf_op jit(solution)/shard_map/stats/pallas_call | solution.py:258
  4.8 20.5 %collective-permute-start = (f32[768,128]{1,0:T(8,128)S(1)}, f32[768,128]{1,0:T(8,128)S(1)}, u32[]{:S(2)}, u32[]{:S(2)}) collective-permute-start(f32[768,128]{1,0:T(8,128)S(1)} %get-tuple-element.5), channel_id=1, source_target_pairs={{0,1},{1,0},{2,3},{3,2},{4,5},{5,4},{6,7},{7,6},{8,9},{9,8},{10,11... | collective-permute-start | bytes 1179656 | tf_op jit(solution)/shard_map/ppermute | solution.py:275
  25.4 1.3 %collective-permute-done = f32[768,128]{1,0:T(8,128)S(1)} collective-permute-done((f32[768,128]{1,0:T(8,128)S(1)}, f32[768,128]{1,0:T(8,128)S(1)}, u32[]{:S(2)}, u32[]{:S(2)}) %collective-permute-start) | collective-permute-done | bytes 393248 | tf_op jit(solution)/shard_map/ppermute | solution.py:275
  26.7 0.1 add.12
  26.8 0.1 collective-permute-start.1
  27.0 3.9 %collective-permute-start.2 = (f32[192,128]{1,0:T(8,128)S(1)}, f32[192,128]{1,0:T(8,128)S(1)}, u32[]{:S(2)}, u32[]{:S(2)}) collective-permute-start(f32[192,128]{1,0:T(8,128)S(1)} %get-tuple-element.9), channel_id=1, source_target_pairs={{0,62},{2,0},{4,2},{6,4},{8,6},{10,8},{12,10},{14,12},{16,14},{18,... | collective-permute-start | bytes 294920 | tf_op jit(solution)/shard_map/ppermute | solution.py:243
  30.8 0.1 collective-permute-start.3
  31.0 3.5 %collective-permute-start.4 = (f32[96,128]{1,0:T(8,128)S(1)}, f32[96,128]{1,0:T(8,128)S(1)}, u32[]{:S(2)}, u32[]{:S(2)}) collective-permute-start(f32[96,128]{1,0:T(8,128)S(1)} %get-tuple-element.7), channel_id=1, source_target_pairs={{0,60},{2,62},{4,0},{6,2},{8,4},{10,6},{12,8},{14,10},{16,12},{18,... | collective-permute-start | bytes 147464 | tf_op jit(solution)/shard_map/ppermute | solution.py:243
  34.5 1.6 %collective-permute-done.3 = f32[96,128]{1,0:T(8,128)S(1)} collective-permute-done((f32[96,128]{1,0:T(8,128)S(1)}, f32[96,128]{1,0:T(8,128)S(1)}, u32[]{:S(2)}, u32[]{:S(2)}) %collective-permute-start.3) | collective-permute-done | bytes 49184 | tf_op jit(solution)/shard_map/ppermute | solution.py:243
  36.2 0.0 collective-permute-done.4
  36.2 0.0 collective-permute-done.1
  36.2 0.0 collective-permute-done.2
  36.2 34.4 %all_to_all.10 = f32[8,24,128]{2,1,0:T(8,128)S(1)} all-to-all(f32[8,24,128]{2,1,0:T(8,128)S(1)} %bitcast.19), channel_id=1, replica_groups=mesh['grp'=4,'far'=8,'near'=4,'core'=2] {'far'}, dimensions={0} | all-to-all | bytes 196608 | tf_op jit(solution)/shard_map/all_to_all | solution.py:282
  70.7 27.8 %all_to_all.11 = f32[8,24,128]{2,1,0:T(8,128)S(1)} all-to-all(f32[8,24,128]{2,1,0:T(8,128)S(1)} %broadcast_in_dim.3), channel_id=1, replica_groups=mesh['grp'=4,'far'=8,'near'=4,'core'=2] {'far'}, dimensions={0} | all-to-all | bytes 196608 | tf_op jit(solution)/shard_map/all_to_all | solution.py:284
  98.4 5.3 %collective-permute-start.9 = (f32[192,128]{1,0:T(8,128)S(1)}, f32[192,128]{1,0:T(8,128)S(1)}, u32[]{:S(2)}, u32[]{:S(2)}) collective-permute-start(f32[192,128]{1,0:T(8,128)S(1)} %bitcast.12), channel_id=1, source_target_pairs={{0,1},{1,0},{2,3},{3,2},{4,5},{5,4},{6,7},{7,6},{8,9},{9,8},{10,11... | collective-permute-start | bytes 294920 | tf_op jit(solution)/shard_map/ppermute | solution.py:286
  103.8 0.4 collective-permute-start.6
  104.2 2.3 %collective-permute-start.5 = (f32[192,128]{1,0:T(8,128)S(1)}, f32[192,128]{1,0:T(8,128)S(1)}, u32[]{:S(2)}, u32[]{:S(2)}) collective-permute-start(f32[192,128]{1,0:T(8,128)S(1)} %bitcast.14), channel_id=1, source_target_pairs={{0,62},{2,0},{4,2},{6,4},{8,6},{10,8},{12,10},{14,12},{16,14},{18,... | collective-permute-start | bytes 294920 | tf_op jit(solution)/shard_map/ppermute | solution.py:243
  106.4 0.7 collective-permute-start.7
  107.1 3.0 %collective-permute-start.8 = (f32[96,128]{1,0:T(8,128)S(1)}, f32[96,128]{1,0:T(8,128)S(1)}, u32[]{:S(2)}, u32[]{:S(2)}) collective-permute-start(f32[96,128]{1,0:T(8,128)S(1)} %bitcast.20), channel_id=1, source_target_pairs={{0,60},{2,62},{4,0},{6,2},{8,4},{10,6},{12,8},{14,10},{16,12},{18,... | collective-permute-start | bytes 147464 | tf_op jit(solution)/shard_map/ppermute | solution.py:243
  110.1 0.0 collective-permute-done.6.refs_2_
  110.1 1.1 collective-permute-start.11
  111.2 0.0 collective-permute-done.5.refs_1_
  111.3 0.1 collective-permute-start.10
  111.4 0.2 collective-permute-done.7.refs_3_
  111.6 1.7 %collective-permute-start.12 = (f32[96,128]{1,0:T(8,128)S(1)}, f32[96,128]{1,0:T(8,128)S(1)}, u32[]{:S(2)}, u32[]{:S(2)}) collective-permute-start(f32[96,128]{1,0:T(8,128)S(1)} %collective-permute-done.7.refs_3_), channel_id=1, source_target_pairs={{0,1},{1,0},{2,3},{3,2},{4,5},{5,4},{6,7},{7,6},{8,9},{9,8},{10,11... | collective-permute-start | bytes 147464 | tf_op jit(solution)/shard_map/ppermute | solution.py:286
  113.3 0.0 collective-permute-done.8.refs_4_
  113.3 0.0 collective-permute-start.13
  113.3 0.9 collective-permute-done.12.refs_8_
  114.2 0.4 collective-permute-done.13.refs_9_
  114.5 0.0 collective-permute-done.9.refs_5_
  114.5 0.0 collective-permute-done.11.refs_7_
  114.6 0.0 collective-permute-done.10.refs_6_
  114.6 10.1 %finish.1 = (f32[1024,256]{1,0:T(8,128)}, f32[4,4]{1,0:T(4,128)}) custom-call(s32[1]{0:T(128)} %bitcast.core_ref, s32[1]{0:T(128)} %bitcast.1.near_ref, f32[192,128]{1,0:T(8,128)S(1)} %bitcast.15, f32[192,128]{1,0:T(8,128)S(1)} %collective-permute-done.5.refs_1_, f32[192,128]{1,0:T(8,128)S(1)} %collective-permute-done.6.refs_2_, ...), custom_call_target="tpu_custom_call" | custom-call | tf_op jit(solution)/shard_map/finish/pallas_call | solution.py:219
  (6 shorter events, 0.1 us)
Async XLA Ops:
  4.8 21.9 %collective-permute-start = (f32[768,128]{1,0:T(8,128)S(1)}, f32[768,128]{1,0:T(8,128)S(1)}, u32[]{:S(2)}, u32[]{:S(2)}) collective-permute-start(f32[768,128]{1,0:T(8,128)S(1)} %get-tuple-element.5), channel_id=1, source_target_pairs={{0,1},{1,0},{2,3},{3,2},{4,5},{5,4},{6,7},{7,6},{8,9},{9,8},{10,11... | collective-permute-start | bytes 1179656 | tf_op jit(solution)/shard_map/ppermute | solution.py:275
  26.8 9.4 %collective-permute-start.1 = (f32[192,128]{1,0:T(8,128)S(1)}, f32[192,128]{1,0:T(8,128)S(1)}, u32[]{:S(2)}, u32[]{:S(2)}) collective-permute-start(f32[192,128]{1,0:T(8,128)S(1)} %get-tuple-element.8), channel_id=1, source_target_pairs={{0,2},{2,4},{4,6},{6,8},{8,10},{10,12},{12,14},{14,16},{16,18},{18... | collective-permute-start | bytes 294920 | tf_op jit(solution)/shard_map/ppermute | solution.py:243
  27.0 9.2 %collective-permute-start.2 = (f32[192,128]{1,0:T(8,128)S(1)}, f32[192,128]{1,0:T(8,128)S(1)}, u32[]{:S(2)}, u32[]{:S(2)}) collective-permute-start(f32[192,128]{1,0:T(8,128)S(1)} %get-tuple-element.9), channel_id=1, source_target_pairs={{0,62},{2,0},{4,2},{6,4},{8,6},{10,8},{12,10},{14,12},{16,14},{18,... | collective-permute-start | bytes 294920 | tf_op jit(solution)/shard_map/ppermute | solution.py:243
  30.8 5.3 %collective-permute-start.3 = (f32[96,128]{1,0:T(8,128)S(1)}, f32[96,128]{1,0:T(8,128)S(1)}, u32[]{:S(2)}, u32[]{:S(2)}) collective-permute-start(f32[96,128]{1,0:T(8,128)S(1)} %get-tuple-element.6), channel_id=1, source_target_pairs={{0,4},{2,6},{4,8},{6,10},{8,12},{10,14},{12,16},{14,18},{16,20},{1... | collective-permute-start | bytes 147464 | tf_op jit(solution)/shard_map/ppermute | solution.py:243
  31.0 5.2 %collective-permute-start.4 = (f32[96,128]{1,0:T(8,128)S(1)}, f32[96,128]{1,0:T(8,128)S(1)}, u32[]{:S(2)}, u32[]{:S(2)}) collective-permute-start(f32[96,128]{1,0:T(8,128)S(1)} %get-tuple-element.7), channel_id=1, source_target_pairs={{0,60},{2,62},{4,0},{6,2},{8,4},{10,6},{12,8},{14,10},{16,12},{18,... | collective-permute-start | bytes 147464 | tf_op jit(solution)/shard_map/ppermute | solution.py:243
  98.4 16.1 %collective-permute-start.9 = (f32[192,128]{1,0:T(8,128)S(1)}, f32[192,128]{1,0:T(8,128)S(1)}, u32[]{:S(2)}, u32[]{:S(2)}) collective-permute-start(f32[192,128]{1,0:T(8,128)S(1)} %bitcast.12), channel_id=1, source_target_pairs={{0,1},{1,0},{2,3},{3,2},{4,5},{5,4},{6,7},{7,6},{8,9},{9,8},{10,11... | collective-permute-start | bytes 294920 | tf_op jit(solution)/shard_map/ppermute | solution.py:286
  103.8 6.4 %collective-permute-start.6 = (f32[192,128]{1,0:T(8,128)S(1)}, f32[192,128]{1,0:T(8,128)S(1)}, u32[]{:S(2)}, u32[]{:S(2)}) collective-permute-start(f32[192,128]{1,0:T(8,128)S(1)} %bitcast.13), channel_id=1, source_target_pairs={{0,2},{2,4},{4,6},{6,8},{8,10},{10,12},{12,14},{14,16},{16,18},{18... | collective-permute-start | bytes 294920 | tf_op jit(solution)/shard_map/ppermute | solution.py:243
  104.2 7.1 %collective-permute-start.5 = (f32[192,128]{1,0:T(8,128)S(1)}, f32[192,128]{1,0:T(8,128)S(1)}, u32[]{:S(2)}, u32[]{:S(2)}) collective-permute-start(f32[192,128]{1,0:T(8,128)S(1)} %bitcast.14), channel_id=1, source_target_pairs={{0,62},{2,0},{4,2},{6,4},{8,6},{10,8},{12,10},{14,12},{16,14},{18,... | collective-permute-start | bytes 294920 | tf_op jit(solution)/shard_map/ppermute | solution.py:243
  106.4 5.2 %collective-permute-start.7 = (f32[96,128]{1,0:T(8,128)S(1)}, f32[96,128]{1,0:T(8,128)S(1)}, u32[]{:S(2)}, u32[]{:S(2)}) collective-permute-start(f32[96,128]{1,0:T(8,128)S(1)} %bitcast.21), channel_id=1, source_target_pairs={{0,4},{2,6},{4,8},{6,10},{8,12},{10,14},{12,16},{14,18},{16,20},{1... | collective-permute-start | bytes 147464 | tf_op jit(solution)/shard_map/ppermute | solution.py:243
  107.1 6.2 %collective-permute-start.8 = (f32[96,128]{1,0:T(8,128)S(1)}, f32[96,128]{1,0:T(8,128)S(1)}, u32[]{:S(2)}, u32[]{:S(2)}) collective-permute-start(f32[96,128]{1,0:T(8,128)S(1)} %bitcast.20), channel_id=1, source_target_pairs={{0,60},{2,62},{4,0},{6,2},{8,4},{10,6},{12,8},{14,10},{16,12},{18,... | collective-permute-start | bytes 147464 | tf_op jit(solution)/shard_map/ppermute | solution.py:243
  110.1 4.4 %collective-permute-start.11 = (f32[192,128]{1,0:T(8,128)S(1)}, f32[192,128]{1,0:T(8,128)S(1)}, u32[]{:S(2)}, u32[]{:S(2)}) collective-permute-start(f32[192,128]{1,0:T(8,128)S(1)} %collective-permute-done.6.refs_2_), channel_id=1, source_target_pairs={{0,1},{1,0},{2,3},{3,2},{4,5},{5,4},{6,7},{7,6},{8,9},{9,8},{10,11... | collective-permute-start | bytes 294920 | tf_op jit(solution)/shard_map/ppermute | solution.py:286
  111.3 3.3 %collective-permute-start.10 = (f32[192,128]{1,0:T(8,128)S(1)}, f32[192,128]{1,0:T(8,128)S(1)}, u32[]{:S(2)}, u32[]{:S(2)}) collective-permute-start(f32[192,128]{1,0:T(8,128)S(1)} %collective-permute-done.5.refs_1_), channel_id=1, source_target_pairs={{0,1},{1,0},{2,3},{3,2},{4,5},{5,4},{6,7},{7,6},{8,9},{9,8},{10,11... | collective-permute-start | bytes 294920 | tf_op jit(solution)/shard_map/ppermute | solution.py:286
  111.6 2.6 %collective-permute-start.12 = (f32[96,128]{1,0:T(8,128)S(1)}, f32[96,128]{1,0:T(8,128)S(1)}, u32[]{:S(2)}, u32[]{:S(2)}) collective-permute-start(f32[96,128]{1,0:T(8,128)S(1)} %collective-permute-done.7.refs_3_), channel_id=1, source_target_pairs={{0,1},{1,0},{2,3},{3,2},{4,5},{5,4},{6,7},{7,6},{8,9},{9,8},{10,11... | collective-permute-start | bytes 147464 | tf_op jit(solution)/shard_map/ppermute | solution.py:286
  113.3 1.2 collective-permute-start.13

commit v5 on v4

--- a/solution.py
+++ b/solution.py
@@ -12,10 +12,9 @@
 LANES = 128
 NEAR = 4
 CORES = 2
-PIECES = 5
+PIECES = 4
 ROW = ("far", "near", "core")
 GRP_ROW = ("grp",) + ROW
-CHIP = ("far", "near")
 SWAP = [(0, 1), (1, 0)]
 NT = (((1,), (1,)), ((), ()))
 TN = (((0,), (0,)), ((), ()))
@@ -66,23 +65,26 @@
 
     @pl.when(step == pl.num_programs(0) - 1)
     def _():
-        core = core_ref[0]
-        for slot in range(NEAR):
-            source = pl.multiple_of(lax.rem(near_ref[0] + slot, NEAR) * quarter, 8)
-            rows = slice(slot * quarter, (slot + 1) * quarter)
-            mine_ref[rows, :] = acc_ref[core, pl.ds(source, quarter), :]
-            theirs_ref[rows, :] = acc_ref[1 - core, pl.ds(source, quarter), :]
-
-
-def piece_rows(quarter):
-    return ((0, 0, quarter), (1, 0, quarter), (3, 0, quarter), (2, 0, quarter // 2), (2, quarter // 2, quarter // 2))
+        core, near = core_ref[0], near_ref[0]
+        for out_ref, at in ((mine_ref, core), (theirs_ref, 1 - core)):
+            for place, slot in enumerate(sent_slots(at)):
+                source = pl.multiple_of(lax.rem(near + slot, NEAR) * quarter, 8)
+                out_ref[place * quarter:(place + 1) * quarter, :] = acc_ref[at, pl.ds(source, quarter), :]
+
+
+def sent_slots(core):
+    return 0, 1 + 2 * core, 2, 3 - 2 * core
+
+
+def received_slots(core):
+    return 0, 3 - 2 * core, 2, 1 + 2 * core
 
 
 def spread_row(x, r):
     return jnp.broadcast_to(x[r:r + 1], x.shape)
 
 
-def factor_block(block, panel=16):
+def factor_block(block, panel=8):
     size = block.shape[0]
     row_at = lax.broadcasted_iota(jnp.int32, (size, size), 0)
     lane_at = lax.broadcasted_iota(jnp.int32, (size, size), 1)
@@ -102,26 +104,40 @@
         steps = []
         for q in range(p, p + high):
             pivots = None
-            for r in range(8):
+            for r in range(0, 8, 2):
                 m = 8 * (q - p) + r
-                pivot = spread_row(cols[q][m], r)
-                pivots = pivot if r == 0 else jnp.where(sub == r, pivot, pivots)
-                inverse = 1.0 / pivot
-                row = spread_row(parts[q], r)
-                heads = {k: spread_row(cols[q][k], r) for k in range(m + 1, panel)}
+                left, right = cols[q][m], cols[q][m + 1]
+                a, b, c = spread_row(left, r), spread_row(right, r), spread_row(right, r + 1)
+                determinant = a * c - b * b
+                inverse = 1.0 / determinant
+                ratio = 1.0 / a
+                second = determinant * ratio
+                pivots = a if r == 0 else jnp.where(sub == r, a, pivots)
+                pivots = jnp.where(sub == r + 1, second, pivots)
+
+                def adjugate(x):
+                    x0, x1 = spread_row(x, r), spread_row(x, r + 1)
+                    return c * x0 - b * x1, a * x1 - b * x0
+
+                row0, row1 = adjugate(parts[q])
+                heads = {k: adjugate(cols[q][k]) for k in range(m + 2, panel)}
+                fixed = spread_row(parts[q], r + 1) - (b * ratio) * spread_row(parts[q], r)
                 for i in range(q, p + high):
-                    col = jnp.where(sub > r, cols[i][m], 0.0) if i == q else cols[i][m]
-                    for k in range(m + 1, panel):
-                        cols[i][k] = cols[i][k] - (col * heads[k]) * inverse
-                    parts[i] = parts[i] - (col * row) * inverse
-                steps.append((row * inverse, {k: heads[k] * inverse for k in heads}))
+                    x0, x1 = cols[i][m], cols[i][m + 1]
+                    if i == q:
+                        x0, x1 = jnp.where(sub > r + 1, x0, 0.0), jnp.where(sub > r + 1, x1, 0.0)
+                    for k, (head0, head1) in heads.items():
+                        cols[i][k] = cols[i][k] - (x0 * head0 + x1 * head1) * inverse
+                    parts[i] = parts[i] - (x0 * row0 + x1 * row1) * inverse
+                parts[q] = jnp.where(sub == r + 1, fixed, parts[q])
+                steps.append((m, row0 * inverse, row1 * inverse, {k: (h0 * inverse, h1 * inverse) for k, (h0, h1) in heads.items()}))
             done.append(parts[q] * lax.rsqrt(pivots))
         for i in range(p + high, count):
             col = cols[i]
-            for m, (row, entries) in enumerate(steps):
-                parts[i] = parts[i] - col[m] * row
-                for k in range(m + 1, panel):
-                    col[k] = col[k] - col[m] * entries[k]
+            for m, row0, row1, heads in steps:
+                parts[i] = parts[i] - (col[m] * row0 + col[m + 1] * row1)
+                for k, (head0, head1) in heads.items():
+                    col[k] = col[k] - (col[m] * head0 + col[m + 1] * head1)
     done = jnp.concatenate(done, axis=0)
     upper = jnp.where(row_at <= lane_at, done[:, :size], 0.0)
     return upper, done[:, size:]
@@ -144,9 +160,9 @@
     core, near = core_ref[0], near_ref[0]
     for side in range(CORES):
         half_at = core if side == 0 else 1 - core
-        for piece, (slot, first, size_at) in enumerate(piece_rows(quarter)):
-            at = pl.multiple_of(lax.rem(near + slot, NEAR) * quarter + first, 8)
-            sums_ref[half_at, pl.ds(at, size_at), :] = parts[side * PIECES + piece][...]
+        for piece, slot in enumerate(received_slots(half_at)):
+            at = pl.multiple_of(lax.rem(near + slot, NEAR) * quarter, 8)
+            sums_ref[half_at, pl.ds(at, quarter), :] = parts[side * PIECES + piece][...]
 
     def lanes_block(block):
         return jnp.concatenate([sums_ref[c, block * half:(block + 1) * half, :] for c in range(CORES)], axis=0)
@@ -155,10 +171,13 @@
     own = jnp.concatenate([lanes_block(basis // LANES + b) for b in range(columns // LANES)], axis=1)
     row_at = lax.broadcasted_iota(jnp.int32, (columns, columns), 0)
     lane_at = lax.broadcasted_iota(jnp.int32, (columns, columns), 1)
-    work_ref[:, :columns] = own - lax.dot_general(
-        coefs, coefs, NT, precision=lax.Precision.HIGHEST, preferred_element_type=jnp.float32
-    )
-    work_ref[:, columns:] = (row_at == lane_at).astype(jnp.float32)
+    gram = own - lax.dot_general(coefs, coefs, NT, precision=lax.Precision.HIGHEST, preferred_element_type=jnp.float32)
+    own_diagonal = jnp.where(row_at == lane_at, own, 0.0)
+    energies = jnp.sum(own_diagonal, axis=0, keepdims=True)
+    scale = lax.rsqrt(energies)
+    scale_down = lax.rsqrt(jnp.sum(own_diagonal, axis=1, keepdims=True))
+    work_ref[:, :columns] = gram * (scale * scale_down)
+    work_ref[:, columns:] = jnp.where(row_at == lane_at, scale, 0.0)
     coefs_s = split(coefs)
     leaf_count = rows // LEAF
 
@@ -187,6 +206,7 @@
     diagonal = jnp.concatenate(
         [jnp.concatenate([uppers[k] if j == k else zero for j in range(rounds)], axis=1) for k in range(rounds)], axis=0
     )
+    diagonal = diagonal * (energies * scale)
     inverse = work_ref[:, columns:]
     inverse_t = split(jnp.where(row_at >= lane_at, inverse, 0.0))
     diagonal_s = split(diagonal)
@@ -204,7 +224,6 @@
     ).astype(jnp.float32)
     leaf_sums = jnp.concatenate(sums + [jnp.zeros((8 - count, columns), jnp.float32)], axis=0)
     leaf_energy = dot4(split(member), split(leaf_sums), NT)
-    energies = jnp.sum(jnp.where(row_at == lane_at, own, 0.0), axis=0, keepdims=True)
     energy = jnp.sum(member * energies, axis=1, keepdims=True)
     est_ref[...] = jnp.sqrt(leaves * leaf_energy / energy)[:rounds, :count]
 
@@ -239,8 +258,12 @@
 
 
 def shifted(x, hops):
-    count = lax.axis_size(CHIP)
-    return lax.ppermute(x, CHIP, [(i, (i + hops) % count) for i in range(count)])
+    chips = lax.axis_size("far") * NEAR
+    pairs = []
+    for chip in range(chips):
+        pairs.append((chip * CORES, (chip + hops) % chips * CORES))
+        pairs.append((chip * CORES + 1, (chip - hops) % chips * CORES + 1))
+    return lax.ppermute(x, ROW, pairs)
 
 
 def local(prior_basis, samples):
@@ -273,16 +296,14 @@
         name="stats",
     )(core, near, prior_basis, samples_t)
     chip = (mine + lax.ppermute(theirs, "core", SWAP)).reshape(NEAR, quarter, LANES)
-    middle = quarter // 2
-    from_left = shifted(chip[1], 1)
-    from_right = shifted(chip[3], -1)
-    from_far_left = shifted(chip[2, :middle], 2)
-    from_far_right = shifted(chip[2, middle:], -2)
-    near_sum = chip[0] + from_left + from_right + jnp.concatenate([from_far_left, from_far_right], axis=0)
+    two_on = shifted(chip[2], 2)
+    one_on = shifted(chip[1], 1)
+    one_back = shifted(chip[3], -1)
+    near_sum = chip[0] + one_on + one_back + two_on
     far_parts = lax.all_to_all(near_sum.reshape(far, quarter // far, LANES), "far", 0, 0, tiled=True)
     total = jnp.sum(far_parts, axis=0)
     own = lax.all_to_all(jnp.broadcast_to(total, far_parts.shape), "far", 0, 0, tiled=True).reshape(quarter, LANES)
-    pieces = [own, shifted(own, -1), shifted(own, 1), shifted(own[:middle], 2), shifted(own[middle:], -2)]
+    pieces = [own, shifted(own, 1), shifted(own, 2), shifted(own, -1)]
     parts = pieces + [lax.ppermute(piece, "core", SWAP) for piece in pieces]
     leaves = float(rows // LEAF * far * NEAR * CORES)
     return run_finish(leaves, core, near, parts, prior_basis, samples_t)

time: 125 us -> 123 us (0.984)
  blocking collectives: 62.2 us -> 59.7 us
  waiting for transfers between devices: 4.46 us -> 6.5 us
    ppermute x8 -> x6, starting transfers between devices: 14 us -> 8.27 us  [shifted(): return lax.ppermute(x, ROW, pairs)]
    ppermute x5 -> x4, starting transfers between devices: 8.3 us -> 13.3 us  [local(): parts = pieces + [lax.ppermute(piece, 'core', SWAP) for piece in pieces]]
    ppermute x8 -> x6, waiting for transfers between devices: 1.88 us -> 4.21 us  [shifted(): return lax.ppermute(x, ROW, pairs)]
    all_to_all x1, blocking collectives: 27.8 us -> 26.4 us  [local(): lax.all_to_all(jnp.broadcast_to(total, far_parts.shape), 'far', 0, 0, til...]
  transfers between devices with their start and end apart: 14 -> 11, of which waited for: 5 -> 4; matrix products, arithmetic and copies ran while one was open for 0% -> 0% of each run, Pallas kernels for 0% -> 0%
where the time goes in v5:
time: 123 us
  blocking collectives  59.7 us (49%)
  starting transfers between devices  42.1 us (34%)
  Pallas kernels  13.5 us (11%)
  waiting for transfers between devices  6.5 us (5%)
    all_to_all x1, blocking collectives, local(): lax.all_to_all(near_sum.reshape(far, quarter // far, LANES), 'far', 0, 0,...  33.3 us
    all_to_all x1, blocking collectives, local(): lax.all_to_all(jnp.broadcast_to(total, far_parts.shape), 'far', 0, 0, til...  26.4 us
    ppermute x1, starting transfers between devices, local(): lax.ppermute(theirs, 'core', SWAP)  20.5 us
    ppermute x4, starting transfers between devices, local(): parts = pieces + [lax.ppermute(piece, 'core', SWAP) for piece in pieces]  13.3 us
    pallas_call x1, Pallas kernels, run_finish(): pl.pallas_call(functools.partial(finish_kernel, leaves), in_specs=[pl.Blo...  9.35 us
    ppermute x6, starting transfers between devices, shifted(): return lax.ppermute(x, ROW, pairs)  8.27 us
    ppermute x6, waiting for transfers between devices, shifted(): return lax.ppermute(x, ROW, pairs)  4.21 us
    pallas_call x1, Pallas kernels, local(): pl.pallas_call(stats_kernel, grid=(rows // step,), in_specs=[pl.BlockSpec...  4.2 us
  transfers between devices with their start and end apart: 11, of which 4 were waited for; matrix products, arithmetic and copies ran while one was open for 0% of the time, Pallas kernels for 0%

profile of v5, /device:TPU:37, one launch (start us, length us, event | category | flops | bytes accessed | tf_op | source)
XLA Modules:
  0.0 122.8 jit_solution(7518920839981610648)
XLA Ops:
  0.6 4.2 %stats.1 = (f32[768,128]{1,0:T(8,128)S(1)}, f32[768,128]{1,0:T(8,128)S(1)}) custom-call(s32[1]{0:T(128)} %bitcast.core_ref, s32[1]{0:T(128)} %bitcast.1.near_ref, f32[1024,512]{1,0:T(8,128)} %refs_8_.1, f32[4,64,1024]{2,1,0:T(8,128)} %bitcast.10), custom_call_target="tpu_custom_call" | custom-call | tf_op jit(solution)/shard_map/stats/pallas_call | solution.py:281
  4.8 20.5 %collective-permute-start = (f32[768,128]{1,0:T(8,128)S(1)}, f32[768,128]{1,0:T(8,128)S(1)}, u32[]{:S(2)}, u32[]{:S(2)}) collective-permute-start(f32[768,128]{1,0:T(8,128)S(1)} %get-tuple-element.5), channel_id=1, source_target_pairs={{0,1},{1,0},{2,3},{3,2},{4,5},{5,4},{6,7},{7,6},{8,9},{9,8},{10,11... | collective-permute-start | bytes 1179656 | tf_op jit(solution)/shard_map/ppermute | solution.py:298
  25.4 1.3 %collective-permute-done = f32[768,128]{1,0:T(8,128)S(1)} collective-permute-done((f32[768,128]{1,0:T(8,128)S(1)}, f32[768,128]{1,0:T(8,128)S(1)}, u32[]{:S(2)}, u32[]{:S(2)}) %collective-permute-start) | collective-permute-done | bytes 393248 | tf_op jit(solution)/shard_map/ppermute | solution.py:298
  26.7 0.1 add.12
  26.8 3.9 %collective-permute-start.1 = (f32[192,128]{1,0:T(8,128)S(1)}, f32[192,128]{1,0:T(8,128)S(1)}, u32[]{:S(2)}, u32[]{:S(2)}) collective-permute-start(f32[192,128]{1,0:T(8,128)S(1)} %get-tuple-element.6), channel_id=1, source_target_pairs={{0,2},{1,63},{2,4},{3,1},{4,6},{5,3},{6,8},{7,5},{8,10},{9,7},{10,... | collective-permute-start | bytes 294920 | tf_op jit(solution)/shard_map/ppermute | solution.py:266
  30.7 0.8 collective-permute-start.3
  31.5 0.9 collective-permute-start.2
  32.4 0.0 collective-permute-done.1
  32.4 3.0 %collective-permute-done.3 = f32[192,128]{1,0:T(8,128)S(1)} collective-permute-done((f32[192,128]{1,0:T(8,128)S(1)}, f32[192,128]{1,0:T(8,128)S(1)}, u32[]{:S(2)}, u32[]{:S(2)}) %collective-permute-start.3) | collective-permute-done | bytes 98336 | tf_op jit(solution)/shard_map/ppermute | solution.py:266
  35.4 1.2 collective-permute-done.2
  36.6 33.3 %all_to_all.10 = f32[8,24,128]{2,1,0:T(8,128)S(1)} all-to-all(f32[8,24,128]{2,1,0:T(8,128)S(1)} %bitcast.12), channel_id=1, replica_groups=mesh['grp'=4,'far'=8,'near'=4,'core'=2] {'far'}, dimensions={0} | all-to-all | bytes 196608 | tf_op jit(solution)/shard_map/all_to_all | solution.py:303
  70.0 26.4 %all_to_all.11 = f32[8,24,128]{2,1,0:T(8,128)S(1)} all-to-all(f32[8,24,128]{2,1,0:T(8,128)S(1)} %broadcast_in_dim.3), channel_id=1, replica_groups=mesh['grp'=4,'far'=8,'near'=4,'core'=2] {'far'}, dimensions={0} | all-to-all | bytes 196608 | tf_op jit(solution)/shard_map/all_to_all | solution.py:305
  96.4 0.0 collective-permute-start.6
  96.4 0.5 collective-permute-start.5
  96.9 2.2 %collective-permute-start.4 = (f32[192,128]{1,0:T(8,128)S(1)}, f32[192,128]{1,0:T(8,128)S(1)}, u32[]{:S(2)}, u32[]{:S(2)}) collective-permute-start(f32[192,128]{1,0:T(8,128)S(1)} %bitcast.7), channel_id=1, source_target_pairs={{0,2},{1,63},{2,4},{3,1},{4,6},{5,3},{6,8},{7,5},{8,10},{9,7},{10,... | collective-permute-start | bytes 294920 | tf_op jit(solution)/shard_map/ppermute | solution.py:266
  99.1 8.5 %collective-permute-start.7 = (f32[192,128]{1,0:T(8,128)S(1)}, f32[192,128]{1,0:T(8,128)S(1)}, u32[]{:S(2)}, u32[]{:S(2)}) collective-permute-start(f32[192,128]{1,0:T(8,128)S(1)} %bitcast.8), channel_id=1, source_target_pairs={{0,1},{1,0},{2,3},{3,2},{4,5},{5,4},{6,7},{7,6},{8,9},{9,8},{10,11... | collective-permute-start | bytes 294920 | tf_op jit(solution)/shard_map/ppermute | solution.py:307
  107.6 0.0 collective-permute-done.6.refs_3_
  107.6 0.0 collective-permute-start.10
  107.6 0.0 collective-permute-done.5.refs_2_
  107.6 2.6 %collective-permute-start.9 = (f32[192,128]{1,0:T(8,128)S(1)}, f32[192,128]{1,0:T(8,128)S(1)}, u32[]{:S(2)}, u32[]{:S(2)}) collective-permute-start(f32[192,128]{1,0:T(8,128)S(1)} %collective-permute-done.5.refs_2_), channel_id=1, source_target_pairs={{0,1},{1,0},{2,3},{3,2},{4,5},{5,4},{6,7},{7,6},{8,9},{9,8},{10,11... | collective-permute-start | bytes 294920 | tf_op jit(solution)/shard_map/ppermute | solution.py:307
  110.3 0.0 collective-permute-done.4.refs_1_
  110.3 2.1 %collective-permute-start.8 = (f32[192,128]{1,0:T(8,128)S(1)}, f32[192,128]{1,0:T(8,128)S(1)}, u32[]{:S(2)}, u32[]{:S(2)}) collective-permute-start(f32[192,128]{1,0:T(8,128)S(1)} %collective-permute-done.4.refs_1_), channel_id=1, source_target_pairs={{0,1},{1,0},{2,3},{3,2},{4,5},{5,4},{6,7},{7,6},{8,9},{9,8},{10,11... | collective-permute-start | bytes 294920 | tf_op jit(solution)/shard_map/ppermute | solution.py:307
  112.3 0.0 collective-permute-done.7.refs_4_
  112.3 0.0 collective-permute-done.10.refs_7_
  112.3 0.0 collective-permute-done.9.refs_6_
  112.3 0.9 collective-permute-done.8.refs_5_
  113.3 9.3 %finish.1 = (f32[1024,256]{1,0:T(8,128)}, f32[4,4]{1,0:T(4,128)}) custom-call(s32[1]{0:T(128)} %bitcast.core_ref, s32[1]{0:T(128)} %bitcast.1.near_ref, f32[192,128]{1,0:T(8,128)S(1)} %bitcast.9, f32[192,128]{1,0:T(8,128)S(1)} %collective-permute-done.4.refs_1_, f32[192,128]{1,0:T(8,128)S(1)} %collective-permute-done.5.refs_2_, ...), custom_call_target="tpu_custom_call" | custom-call | tf_op jit(solution)/shard_map/finish/pallas_call | solution.py:238
  (4 shorter events, 0.1 us)
Async XLA Ops:
  4.8 21.9 %collective-permute-start = (f32[768,128]{1,0:T(8,128)S(1)}, f32[768,128]{1,0:T(8,128)S(1)}, u32[]{:S(2)}, u32[]{:S(2)}) collective-permute-start(f32[768,128]{1,0:T(8,128)S(1)} %get-tuple-element.5), channel_id=1, source_target_pairs={{0,1},{1,0},{2,3},{3,2},{4,5},{5,4},{6,7},{7,6},{8,9},{9,8},{10,11... | collective-permute-start | bytes 1179656 | tf_op jit(solution)/shard_map/ppermute | solution.py:298
  26.8 5.6 %collective-permute-start.1 = (f32[192,128]{1,0:T(8,128)S(1)}, f32[192,128]{1,0:T(8,128)S(1)}, u32[]{:S(2)}, u32[]{:S(2)}) collective-permute-start(f32[192,128]{1,0:T(8,128)S(1)} %get-tuple-element.6), channel_id=1, source_target_pairs={{0,2},{1,63},{2,4},{3,1},{4,6},{5,3},{6,8},{7,5},{8,10},{9,7},{10,... | collective-permute-start | bytes 294920 | tf_op jit(solution)/shard_map/ppermute | solution.py:266
  30.7 4.7 %collective-permute-start.3 = (f32[192,128]{1,0:T(8,128)S(1)}, f32[192,128]{1,0:T(8,128)S(1)}, u32[]{:S(2)}, u32[]{:S(2)}) collective-permute-start(f32[192,128]{1,0:T(8,128)S(1)} %get-tuple-element.7), channel_id=1, source_target_pairs={{0,4},{1,61},{2,6},{3,63},{4,8},{5,1},{6,10},{7,3},{8,12},{9,5},{1... | collective-permute-start | bytes 294920 | tf_op jit(solution)/shard_map/ppermute | solution.py:266
  31.5 5.1 %collective-permute-start.2 = (f32[192,128]{1,0:T(8,128)S(1)}, f32[192,128]{1,0:T(8,128)S(1)}, u32[]{:S(2)}, u32[]{:S(2)}) collective-permute-start(f32[192,128]{1,0:T(8,128)S(1)} %get-tuple-element.8), channel_id=1, source_target_pairs={{0,62},{1,3},{2,0},{3,5},{4,2},{5,7},{6,4},{7,9},{8,6},{9,11},{10,... | collective-permute-start | bytes 294920 | tf_op jit(solution)/shard_map/ppermute | solution.py:266
  96.4 11.2 %collective-permute-start.6 = (f32[192,128]{1,0:T(8,128)S(1)}, f32[192,128]{1,0:T(8,128)S(1)}, u32[]{:S(2)}, u32[]{:S(2)}) collective-permute-start(f32[192,128]{1,0:T(8,128)S(1)} %bitcast.5), channel_id=1, source_target_pairs={{0,62},{1,3},{2,0},{3,5},{4,2},{5,7},{6,4},{7,9},{8,6},{9,11},{10,... | collective-permute-start | bytes 294920 | tf_op jit(solution)/shard_map/ppermute | solution.py:266
  96.4 11.2 %collective-permute-start.5 = (f32[192,128]{1,0:T(8,128)S(1)}, f32[192,128]{1,0:T(8,128)S(1)}, u32[]{:S(2)}, u32[]{:S(2)}) collective-permute-start(f32[192,128]{1,0:T(8,128)S(1)} %bitcast.6), channel_id=1, source_target_pairs={{0,4},{1,61},{2,6},{3,63},{4,8},{5,1},{6,10},{7,3},{8,12},{9,5},{1... | collective-permute-start | bytes 294920 | tf_op jit(solution)/shard_map/ppermute | solution.py:266
  96.9 13.4 %collective-permute-start.4 = (f32[192,128]{1,0:T(8,128)S(1)}, f32[192,128]{1,0:T(8,128)S(1)}, u32[]{:S(2)}, u32[]{:S(2)}) collective-permute-start(f32[192,128]{1,0:T(8,128)S(1)} %bitcast.7), channel_id=1, source_target_pairs={{0,2},{1,63},{2,4},{3,1},{4,6},{5,3},{6,8},{7,5},{8,10},{9,7},{10,... | collective-permute-start | bytes 294920 | tf_op jit(solution)/shard_map/ppermute | solution.py:266
  99.1 13.3 %collective-permute-start.7 = (f32[192,128]{1,0:T(8,128)S(1)}, f32[192,128]{1,0:T(8,128)S(1)}, u32[]{:S(2)}, u32[]{:S(2)}) collective-permute-start(f32[192,128]{1,0:T(8,128)S(1)} %bitcast.8), channel_id=1, source_target_pairs={{0,1},{1,0},{2,3},{3,2},{4,5},{5,4},{6,7},{7,6},{8,9},{9,8},{10,11... | collective-permute-start | bytes 294920 | tf_op jit(solution)/shard_map/ppermute | solution.py:307
  107.6 4.7 %collective-permute-start.10 = (f32[192,128]{1,0:T(8,128)S(1)}, f32[192,128]{1,0:T(8,128)S(1)}, u32[]{:S(2)}, u32[]{:S(2)}) collective-permute-start(f32[192,128]{1,0:T(8,128)S(1)} %collective-permute-done.6.refs_3_), channel_id=1, source_target_pairs={{0,1},{1,0},{2,3},{3,2},{4,5},{5,4},{6,7},{7,6},{8,9},{9,8},{10,11... | collective-permute-start | bytes 294920 | tf_op jit(solution)/shard_map/ppermute | solution.py:307
  107.6 4.7 %collective-permute-start.9 = (f32[192,128]{1,0:T(8,128)S(1)}, f32[192,128]{1,0:T(8,128)S(1)}, u32[]{:S(2)}, u32[]{:S(2)}) collective-permute-start(f32[192,128]{1,0:T(8,128)S(1)} %collective-permute-done.5.refs_2_), channel_id=1, source_target_pairs={{0,1},{1,0},{2,3},{3,2},{4,5},{5,4},{6,7},{7,6},{8,9},{9,8},{10,11... | collective-permute-start | bytes 294920 | tf_op jit(solution)/shard_map/ppermute | solution.py:307
  110.3 3.0 %collective-permute-start.8 = (f32[192,128]{1,0:T(8,128)S(1)}, f32[192,128]{1,0:T(8,128)S(1)}, u32[]{:S(2)}, u32[]{:S(2)}) collective-permute-start(f32[192,128]{1,0:T(8,128)S(1)} %collective-permute-done.4.refs_1_), channel_id=1, source_target_pairs={{0,1},{1,0},{2,3},{3,2},{4,5},{5,4},{6,7},{7,6},{8,9},{9,8},{10,11... | collective-permute-start | bytes 294920 | tf_op jit(solution)/shard_map/ppermute | solution.py:307
